TPU v7x, 32 devices: a whole 2x2x4 slice. The times are simulated.
32 devices in a mesh: dp: 8 (over z, x), seq: 4 (over y, core).
Axes of the slice: x: 2, y: 2, z: 4, core: 2. Of those that a mesh axis runs over, the one named last changes fastest.
Arguments:
- tokens: bfloat16 [24, 1024, 768], P('dp', 'seq'), may hold values from -6 to 6
- lengths: int32 [24], P('dp'), may hold values from 256 to 1024, as said below
- w_qkv: bfloat16 [768, 2304], P(('dp', 'seq')), may hold values from -0.21875 to 0.21875
- w_att_out: bfloat16 [768, 768], P(('dp', 'seq')), may hold values from -1.25 to 1.25
- w_ffin: bfloat16 [768, 4096], P(('dp', 'seq')), may hold values from -0.21875 to 0.21875
- w_ffout: bfloat16 [2048, 768], P(('dp', 'seq')), may hold values from -0.125 to 0.125
- cotangent: bfloat16 [24, 1024, 768], P('dp', 'seq'), may hold values from -6 to 6
Outputs:
- block_output: bfloat16 [24, 1024, 768], P('dp', 'seq')
- grad_tokens: float32 [24, 1024, 768], P('dp', 'seq')
- grad_qkv: float32 [768, 2304], P(('dp', 'seq'))
- grad_att_out: float32 [768, 768], P(('dp', 'seq'))
- grad_ffin: float32 [768, 4096], P(('dp', 'seq'))
- grad_ffout: float32 [2048, 768], P(('dp', 'seq'))
Inputs may be any that keep to these rules, and one draw needn't show every extreme that they name: `lengths`: some slot has length exactly 1024 and another exactly 256.
All inputs are finite; a program needn't handle non-finite values.
Results may differ from a plain program's by a relative error of at most 0.014.
Values may be sent and summed in bfloat16 or wider, within the bound.
A program may use at most 192 MiB of HBM per device.

v0:
```python
import jax
import jax.numpy as jnp
from jax import lax
from jax.sharding import PartitionSpec as P

HEAD_DIM = 64


def norm_rows(values):
    centred = values - jnp.mean(values, axis=-1, keepdims=True)
    spread = jnp.mean(centred * centred, axis=-1, keepdims=True)
    inverse = lax.rsqrt(spread + 1e-05)
    return (centred * inverse, inverse)


def norm_back(grad_in, normed, inverse):
    mean_grad = jnp.mean(grad_in, axis=-1, keepdims=True)
    mean_prod = jnp.mean(grad_in * normed, axis=-1, keepdims=True)
    return (grad_in - mean_grad - normed * mean_prod) * inverse


def rope_tables(positions):
    exponent = jnp.arange(HEAD_DIM // 2, dtype=jnp.float32) * (2.0 / HEAD_DIM)
    frequency = 10000.0 ** (-exponent)
    angles = positions.astype(jnp.float32)[:, None] * frequency[None, :]
    cosine = jnp.concatenate([jnp.cos(angles), jnp.cos(angles)], -1)
    sine_table = jnp.concatenate([jnp.sin(angles), jnp.sin(angles)], -1)
    return (cosine[None, :, None, :], sine_table[None, :, None, :])


def rotate(values, cosine, sine_table):
    half_dim = values.shape[-1] // 2
    turned = jnp.concatenate([-values[..., half_dim:], values[..., :half_dim]], -1)
    return values * cosine + turned * sine_table


def rotate_back(grad_in, cosine, sine_table):
    half_dim = grad_in.shape[-1] // 2
    scaled = grad_in * sine_table
    return grad_in * cosine + jnp.concatenate([scaled[..., half_dim:], -scaled[..., :half_dim]], -1)


def contract_last(left_side, right_side):
    return lax.dot_general(
        left_side, right_side, (((1,), (1,)), ((), ())), preferred_element_type=jnp.float32
    )


def attention_weights(w_qkv, w_att_out):
    model_width = w_att_out.shape[1]
    packed = jnp.concatenate([w_qkv.reshape(-1, model_width), w_att_out], 0)
    gathered = lax.all_gather(packed, ("dp", "seq"), axis=0, tiled=True)
    devices = gathered.shape[0] // packed.shape[0]
    gathered = gathered.reshape(devices, packed.shape[0], model_width)
    split_rows = w_qkv.shape[0] * w_qkv.shape[1] // model_width
    return (
        gathered[:, :split_rows].reshape(-1, w_qkv.shape[1]),
        gathered[:, split_rows:].reshape(-1, model_width),
    )


def ffn_weights(w_ffin, w_ffout):
    model_width = w_ffout.shape[1]
    packed = jnp.concatenate([w_ffin.reshape(-1, model_width), w_ffout], 0)
    gathered = lax.all_gather(packed, ("dp", "seq"), axis=0, tiled=True)
    devices = gathered.shape[0] // packed.shape[0]
    gathered = gathered.reshape(devices, packed.shape[0], model_width)
    split_rows = w_ffin.shape[0] * w_ffin.shape[1] // model_width
    return (
        gathered[:, :split_rows].reshape(-1, w_ffin.shape[1]),
        gathered[:, split_rows:].reshape(-1, model_width),
    )


def block_terms(term_pairs, packed_rows, model_width, row_span):
    blocks = row_span // packed_rows
    term_parts = []
    for left_side, right_side, share_rows in term_pairs:
        term_piece = lax.dot_general(
            left_side, right_side, (((0,), (0,)), ((), ())), preferred_element_type=jnp.float32
        )
        term_parts.append(term_piece.reshape(blocks, -1, model_width))
    return jnp.concatenate(term_parts, 1).reshape(row_span, model_width)


def on_device(tokens, lengths, w_qkv, w_att_out, w_ffin, w_ffout, cotangent):
    slot_count, local_len, model_width = tokens.shape
    head_count = model_width // HEAD_DIM
    row_count = slot_count * local_len
    slot_len = local_len * lax.axis_size("seq")
    positions = lax.axis_index("seq") * local_len + jnp.arange(local_len, dtype=jnp.int32)
    key_positions = jnp.arange(slot_len, dtype=jnp.int32)
    valid_rows = (positions[None, :] < lengths[:, None]).astype(jnp.float32)[:, :, None]
    cosine, sine_table = rope_tables(positions)
    score_scale = HEAD_DIM ** (-0.5)

    def masked_scores(query_one, key_one, length):
        allowed = (key_positions[None, :] <= positions[:, None]) & (key_positions[None, :] < length)
        raw_scores = (
            jnp.einsum("qhd,khd->hqk", query_one, key_one, preferred_element_type=jnp.float32)
            * score_scale
        )
        return jnp.where(allowed[None], raw_scores, -1e30)

    def forward_slot(item):
        query_one, key_one, value_one, length = item
        scores = masked_scores(query_one, key_one, length)
        row_top = jnp.max(scores, axis=-1, keepdims=True)
        exponent_terms = jnp.exp(scores - row_top)
        row_total = jnp.sum(exponent_terms, axis=-1, keepdims=True)
        probs_bf = (exponent_terms / row_total).astype(jnp.bfloat16)
        mixed_one = jnp.einsum(
            "hqk,khd->qhd", probs_bf, value_one, preferred_element_type=jnp.float32
        )
        return (mixed_one.astype(jnp.bfloat16), row_top + jnp.log(row_total))

    def backward_slot(item):
        query_one, key_one, value_one, grad_mixed_one, log_one, length = item
        probs_again = jnp.exp(masked_scores(query_one, key_one, length) - log_one)
        probs_again_bf = probs_again.astype(jnp.bfloat16)
        grad_probs = jnp.einsum(
            "qhd,khd->hqk", grad_mixed_one, value_one, preferred_element_type=jnp.float32
        )
        grad_scores = probs_again * (
            grad_probs - jnp.sum(probs_again * grad_probs, axis=-1, keepdims=True)
        )
        grad_scores_bf = grad_scores.astype(jnp.bfloat16)
        grad_query_one = (
            jnp.einsum("hqk,khd->qhd", grad_scores_bf, key_one, preferred_element_type=jnp.float32)
            * score_scale
        )
        grad_key_one = (
            jnp.einsum(
                "hqk,qhd->khd", grad_scores_bf, query_one, preferred_element_type=jnp.float32
            )
            * score_scale
        )
        grad_value_one = jnp.einsum(
            "hqk,qhd->khd", probs_again_bf, grad_mixed_one, preferred_element_type=jnp.float32
        )
        return (grad_query_one, grad_key_one, grad_value_one)

    inputs = tokens.astype(jnp.float32).reshape(row_count, model_width)
    normed_one, inverse_one = norm_rows(inputs)
    normed_one_bf = normed_one.astype(jnp.bfloat16)
    qkv_full, att_out_full = attention_weights(w_qkv, w_att_out)
    project = jnp.dot(normed_one_bf, qkv_full, preferred_element_type=jnp.float32)
    project = project.reshape(slot_count, local_len, 3, head_count, HEAD_DIM)
    query_bf = rotate(project[:, :, 0], cosine, sine_table).astype(jnp.bfloat16)
    key_bf = rotate(project[:, :, 1], cosine, sine_table).astype(jnp.bfloat16)
    value_bf = project[:, :, 2].astype(jnp.bfloat16)
    key_all, value_all = (
        lax.all_gather(key_bf, "seq", axis=1, tiled=True),
        lax.all_gather(value_bf, "seq", axis=1, tiled=True),
    )
    mixed_slots, log_total = lax.map(forward_slot, (query_bf, key_all, value_all, lengths))
    mixed_bf = mixed_slots.reshape(row_count, model_width)
    hidden_state = inputs + jnp.dot(mixed_bf, att_out_full, preferred_element_type=jnp.float32)
    normed_two, inverse_two = norm_rows(hidden_state)
    normed_two_bf = normed_two.astype(jnp.bfloat16)
    ffin_full, ffout_full = ffn_weights(w_ffin, w_ffout)
    gate_up = jnp.dot(normed_two_bf, ffin_full, preferred_element_type=jnp.float32)
    half_units = gate_up.shape[1] // 2
    up_part = gate_up[:, :half_units]
    gate_part = gate_up[:, half_units:]
    gate_sigmoid = jax.nn.sigmoid(gate_part)
    activated_bf = (gate_part * gate_sigmoid * up_part).astype(jnp.bfloat16)
    branch = jnp.dot(activated_bf, ffout_full, preferred_element_type=jnp.float32)
    block_output = (valid_rows * (hidden_state + branch).reshape(tokens.shape)).astype(jnp.bfloat16)
    grad_out = (valid_rows * cotangent.astype(jnp.float32)).reshape(row_count, model_width)
    grad_out_bf = grad_out.astype(jnp.bfloat16)
    ffin_back, ffout_back = ffn_weights(w_ffin, w_ffout)
    grad_act = contract_last(grad_out_bf, ffout_back)
    grad_up = grad_act * gate_part * gate_sigmoid
    grad_gate = grad_act * up_part * gate_sigmoid * (1.0 + gate_part * (1.0 - gate_sigmoid))
    grad_gate_up_bf = jnp.concatenate([grad_up, grad_gate], 1).astype(jnp.bfloat16)
    ffn_pairs = (
        (normed_two_bf, grad_gate_up_bf, w_ffin.shape[0]),
        (activated_bf, grad_out_bf, w_ffout.shape[0]),
    )
    ffn_rows = w_ffin.shape[0] * w_ffin.shape[1] // model_width + w_ffout.shape[0]
    att_rows = w_qkv.shape[0] * w_qkv.shape[1] // model_width + w_att_out.shape[0]
    grad_normed_two = contract_last(grad_gate_up_bf, ffin_back)
    grad_hidden = grad_out + norm_back(grad_normed_two, normed_two, inverse_two)
    grad_hidden_bf = grad_hidden.astype(jnp.bfloat16)
    qkv_back, att_out_back = attention_weights(w_qkv, w_att_out)
    grad_mixed_bf = contract_last(grad_hidden_bf, att_out_back).astype(jnp.bfloat16)
    grad_mixed_bf = grad_mixed_bf.reshape(slot_count, local_len, head_count, HEAD_DIM)
    key_use, value_use = (key_all, value_all)
    grad_query, grad_key_all, grad_value_all = lax.map(
        backward_slot, (query_bf, key_use, value_use, grad_mixed_bf, log_total, lengths)
    )
    grad_key, grad_value = (
        lax.psum_scatter(
            grad_key_all.astype(jnp.bfloat16), "seq", scatter_dimension=1, tiled=True
        ).astype(jnp.float32),
        lax.psum_scatter(
            grad_value_all.astype(jnp.bfloat16), "seq", scatter_dimension=1, tiled=True
        ).astype(jnp.float32),
    )
    grad_project_bf = jnp.stack(
        [
            rotate_back(grad_query, cosine, sine_table),
            rotate_back(grad_key, cosine, sine_table),
            grad_value,
        ],
        2,
    )
    grad_project_bf = grad_project_bf.reshape(row_count, 3 * model_width).astype(jnp.bfloat16)
    grad_normed_one = contract_last(grad_project_bf, qkv_back)
    grad_tokens = grad_hidden + norm_back(grad_normed_one, normed_one, inverse_one)
    att_pairs = (
        (normed_one_bf, grad_project_bf, w_qkv.shape[0]),
        (mixed_bf, grad_hidden_bf, w_att_out.shape[0]),
    )
    all_pairs = att_pairs + ffn_pairs
    all_rows = att_rows + ffn_rows
    whole_block = lax.psum_scatter(
        block_terms(all_pairs, all_rows, model_width, lax.axis_size(("dp", "seq")) * all_rows),
        ("dp", "seq"),
        scatter_dimension=0,
        tiled=True,
    )
    att_block = whole_block[:att_rows]
    ffn_block = whole_block[att_rows:]
    qkv_rows = att_rows - w_att_out.shape[0]
    ffin_rows = ffn_rows - w_ffout.shape[0]
    grad_qkv = att_block[:qkv_rows].reshape(w_qkv.shape)
    grad_att_out = att_block[qkv_rows:]
    grad_ffin = ffn_block[:ffin_rows].reshape(w_ffin.shape)
    grad_ffout = ffn_block[ffin_rows:]
    return (
        block_output,
        grad_tokens.reshape(tokens.shape),
        grad_qkv,
        grad_att_out,
        grad_ffin,
        grad_ffout,
    )


def solution(mesh):
    placed = (
        P("dp", "seq", None),
        P("dp"),
        P(("dp", "seq"), None),
        P(("dp", "seq"), None),
        P(("dp", "seq"), None),
        P(("dp", "seq"), None),
        P("dp", "seq", None),
    )
    return jax.shard_map(
        on_device,
        mesh=mesh,
        in_specs=placed,
        out_specs=(
            P("dp", "seq", None),
            P("dp", "seq", None),
            P(("dp", "seq"), None),
            P(("dp", "seq"), None),
            P(("dp", "seq"), None),
            P(("dp", "seq"), None),
        ),
        check_vma=False,
    )
```

profile of v0, /device:TPU:10, one launch (start us, length us, event | category | flops | bytes accessed | tf_op | source)
XLA Modules:
  0.0 832.8 jit_solution(1067020667156078319)
XLA Ops:
  13.8 62.2 %all-gather.6.cloned.1.call-done = bf16[3072,768]{1,0:T(8,128)(2,1)} async-done(((bf16[96,768]{1,0:T(8,128)(2,1)}), bf16[3072,768]{1,0:T(8,128)(2,1)}) %all-gather.6.cloned.1.call-update) | async-done | bytes 4718608 | tf_op jit(solution)/shard_map/all_gather | solution.py:52
  80.0 5.1 reshape.345
  89.1 5.4 fusion.95
  112.4 22.7 %all-gather.12.cloned.1.call-done = bf16[3,1024,1,12,64]{1,4,3,2,0:T(8,128)(2,1)} async-done(((bf16[3,256,1,12,64]{1,4,3,2,0:T(8,128)(2,1)}), bf16[3,1024,1,12,64]{1,4,3,2,0:T(8,128)(2,1)}) %all-gather.12.cloned.1.call-update) | async-done | bytes 4718608 | tf_op jit(solution)/shard_map/all_gather | solution.py:154
  135.2 39.6 %all-gather.8.cloned.1.call-done = bf16[3,1024,12,64]{1,3,2,0:T(8,128)(2,1)} async-done(((bf16[3,256,12,64]{1,3,2,0:T(8,128)(2,1)}), bf16[3,1024,12,64]{1,3,2,0:T(8,128)(2,1)}) %all-gather.8.cloned.1.call-update) | async-done | bytes 4718608 | tf_op jit(solution)/shard_map/all_gather | solution.py:153
  174.8 43.7 %while.30 = (s32[]{:T(128)}, bf16[3,256,12,64]{1,3,2,0:T(8,128)(2,1)S(1)}, f32[3,12,256,1]{2,1,3,0:T(8,128)}, bf16[3,1024,12,64]{1,3,2,0:T(8,128)(2,1)}, s32[3]{...) while((s32[]{:T(128)}, ...), condition=%wide.region_5.6_spmd.clone.clone, body=%wide.region_2.5_spmd.clone.clone.sunk | while | flops 843774208 | bytes 42846332 | solution.py:156
  183.6 5.1 fusion.154
  198.2 5.1 fusion.154
  212.8 5.1 fusion.154
  221.8 37.6 %all-gather.10.cloned.1.call-done = bf16[6144,768]{1,0:T(8,128)(2,1)} async-done(((bf16[192,768]{1,0:T(8,128)(2,1)}), bf16[6144,768]{1,0:T(8,128)(2,1)}) %all-gather.10.cloned.1.call-update) | async-done | bytes 9437200 | tf_op jit(solution)/shard_map/all_gather | solution.py:65
  259.4 6.1 slice.104
  269.4 12.3 %reshape.350 = bf16[768,4096]{1,0:T(8,128)(2,1)} reshape(bf16[32,128,768]{2,1,0:T(8,128)(2,1)} %slice.104) | data formatting | bytes 12582912 | tf_op jit(solution)/shard_map/reshape | solution.py:70
  281.7 11.6 %fusion.106 = f32[768,4096]{1,0:T(8,128)} fusion(bf16[768,4096]{1,0:T(8,128)(2,1)} %reshape.350, f32[768,768]{1,0:T(8,128)S(1)} %get-tuple-element.317, f32[768]{0:T(1024)S(1)} %add_rsqrt_fusion, f32[768]{0:T(1024)S(1)} %broadcast_multiply_fusion.5), kind=kOutput, calls=%fused_computation.151 | convolution fusion | flops 4833607680 | bytes 21239808 | tf_op jit(solution)/shard_map/dot_general | solution.py:162
  293.3 9.3 %multiply_convert_fusion.2 = (bf16[768,2048]{1,0:T(8,128)(2,1)S(1)}, bf16[768,2048]{1,0:T(8,128)(2,1)S(1)}, bf16[768,2048]{1,0:T(8,128)(2,1)}) fusion(f32[768,4096]{1,0:T(8,128)} %fusion.106, bf16[768,768]{1,0:T(8,128)(2,1)S(1)} %bitcast.234, bf16[2048,768]{1,0:T(8,128)(2,1)S(1)} %bitcast.225), kind=kOutput, calls=%fused_computation.72 | convolution fusion | flops 2441084928 | bytes 26345472 | tf_op jit(solution)/shard_map/dot_general | solution.py:44
  302.6 6.6 fusion.109
  317.3 4.7 copy.20
  322.1 94.5 %while.31 = (s32[]{:T(128)}, f32[3,256,12,64]{1,3,2,0:T(8,128)S(1)}, bf16[3,1024,12,64]{1,3,2,0:T(8,128)(2,1)}, bf16[3,1024,12,64]{1,3,2,0:T(8,128)(2,1)}, bf16[...) while((s32[]{:T(128)}, ...), condition=%wide.region_12.13_spmd.clone.clone, body=%wide.region_10.12_spmd.clone.clone.sunk | while | flops 2061957376 | bytes 113611952 | solution.py:190
  327.8 8.9 %multiply_reduce_fusion.4 = (f32[12,256]{1,0:T(8,128)S(1)}, f32[12,256,1024]{2,1,0:T(8,128)}) fusion(f32[12,256,1024]{2,1,0:T(8,128)S(1)} %fusion.163, f32[12,256]{1,0:T(8,128)S(1)} %dynamic-slice_bitcast_fusion.2, pred[256,1024]{1,0:T(8,128)(4,1)S(1)} %fusion.164, bf16[3,1024,12,64]{1,3,2,0:T(8,128)(2,1)} %get-tuple-element.508, s32[]{:T(128)S(6)} %copy.47, ...), kind=kOutput, calls=%fused_computation.30.clone.1 | convolution fusion | flops 418378752 | bytes 27423744 | tf_op jit(solution)/shard_map/while/body/eval_jaxpr/qhd,khd->hqk/dot_general | solution.py:121
  336.7 6.7 multiply_convert_fusion.6
  359.2 8.9 %multiply_reduce_fusion.4 = (f32[12,256]{1,0:T(8,128)S(1)}, f32[12,256,1024]{2,1,0:T(8,128)}) fusion(f32[12,256,1024]{2,1,0:T(8,128)S(1)} %fusion.163, f32[12,256]{1,0:T(8,128)S(1)} %dynamic-slice_bitcast_fusion.2, pred[256,1024]{1,0:T(8,128)(4,1)S(1)} %fusion.164, bf16[3,1024,12,64]{1,3,2,0:T(8,128)(2,1)} %get-tuple-element.508, s32[]{:T(128)S(6)} %copy.47, ...), kind=kOutput, calls=%fused_computation.30.clone.1 | convolution fusion | flops 418378752 | bytes 27423744 | tf_op jit(solution)/shard_map/while/body/eval_jaxpr/qhd,khd->hqk/dot_general | solution.py:121
  368.1 6.7 multiply_convert_fusion.6
  390.7 8.9 %multiply_reduce_fusion.4 = (f32[12,256]{1,0:T(8,128)S(1)}, f32[12,256,1024]{2,1,0:T(8,128)}) fusion(f32[12,256,1024]{2,1,0:T(8,128)S(1)} %fusion.163, f32[12,256]{1,0:T(8,128)S(1)} %dynamic-slice_bitcast_fusion.2, pred[256,1024]{1,0:T(8,128)(4,1)S(1)} %fusion.164, bf16[3,1024,12,64]{1,3,2,0:T(8,128)(2,1)} %get-tuple-element.508, s32[]{:T(128)S(6)} %copy.47, ...), kind=kOutput, calls=%fused_computation.30.clone.1 | convolution fusion | flops 418378752 | bytes 27423744 | tf_op jit(solution)/shard_map/while/body/eval_jaxpr/qhd,khd->hqk/dot_general | solution.py:121
  399.6 6.7 multiply_convert_fusion.6
  418.6 5.1 copy.22
  423.8 14.0 %fusion.72 = f32[768,4096]{1,0:T(8,128)} fusion(bf16[768,2048]{1,0:T(8,128)(2,1)} %copy-done.23, bf16[768,2048]{1,0:T(8,128)(2,1)} %copy-done.22, f32[768,768]{1,0:T(8,128)S(1)} %copy-done.1, f32[768]{0:T(1024)S(1)} %copy-done.38, f32[768]{0:T(1024)S(1)} %copy-done.35), kind=kOutput, calls=%fused_computation.75 | convolution fusion | flops 4846190592 | bytes 21239808 | tf_op jit(solution)/shard_map/dot_general | solution.py:79
  437.7 14.5 %reshape.357 = f32[32,128,768]{2,1,0:T(8,128)} reshape(f32[768,4096]{1,0:T(8,128)} %fusion.72) | data formatting | bytes 25165824 | tf_op jit(solution)/shard_map/reshape | solution.py:82
  470.1 43.4 %reduce-scatter.6.cloned.1.call-done = bf16[3,256,12,64]{1,3,2,0:T(8,128)(2,1)} async-done(((bf16[3,1024,12,64]{1,3,2,0:T(8,128)(2,1)}), bf16[3,256,12,64]{1,3,2,0:T(8,128)(2,1)}) %reduce-scatter.6.cloned.1.call-update) | async-done | bytes 1179664 | tf_op jit(solution)/shard_map/reduce_scatter | solution.py:197
  521.8 5.0 fusion.113
  526.8 8.4 %reshape.356 = f32[32,72,768]{2,1,0:T(8,128)} reshape(f32[768,2304]{1,0:T(8,128)} %fusion.113) | data formatting | bytes 14155776 | tf_op jit(solution)/shard_map/reshape | solution.py:82
  535.2 20.4 %pad_maximum_fusion = f32[32,288,768]{2,1,0:T(8,128)} fusion(f32[32,64,768]{2,1,0:T(8,128)} %fusion.114, f32[32,128,768]{2,1,0:T(8,128)} %reshape.357, f32[32,24,768]{2,1,0:T(8,128)} %fusion.97, f32[32,72,768]{2,1,0:T(8,128)} %reshape.356), kind=kLoop, calls=%fused_computation.69 | loop fusion | flops 21233664 | bytes 56623104 | tf_op jit(solution)/shard_map/concatenate | solution.py:83
  556.3 5.6 convolution_add_fusion
  569.2 249.5 %reduce-scatter.8.cloned.1.call-done = f32[288,768]{1,0:T(8,128)} async-done(((f32[9216,768]{1,0:T(8,128)}), f32[288,768]{1,0:T(8,128)}) %reduce-scatter.8.cloned.1.call-update) | async-done | bytes 884752 | tf_op jit(solution)/shard_map/reduce_scatter | solution.py:218
  (233 shorter events, 166.0 us)
Async XLA Ops:
  7.2 4.1 copy-start.4
  7.2 68.9 %all-gather.6.cloned.1.call-start = ((), (), s32[]{:S(2)}) async-start(), calls=%async_computation.3 | async-start | bytes 4866048 | tf_op jit(solution)/shard_map/all_gather | solution.py:52
  9.7 125.4 %all-gather.12.cloned.1.call-start = ((), (), s32[]{:S(2)}) async-start(), calls=%async_computation.9 | async-start | bytes 5898240 | tf_op jit(solution)/shard_map/all_gather | solution.py:154
  98.5 76.3 %all-gather.8.cloned.1.call-start = ((), (), s32[]{:S(2)}) async-start(), calls=%async_computation.4 | async-start | bytes 5898240 | tf_op jit(solution)/shard_map/all_gather | solution.py:153
  106.4 153.0 %all-gather.10.cloned.1.call-start = ((), (), s32[]{:S(2)}) async-start(), calls=%async_computation.5 | async-start | bytes 9732096 | tf_op jit(solution)/shard_map/all_gather | solution.py:65
  107.5 355.8 %reduce-scatter.4.cloned.1.call-start = ((), (), s32[]{:S(2)}) async-start(), calls=%async_computation.6 | async-start | bytes 5898240 | tf_op jit(solution)/shard_map/reduce_scatter | solution.py:194
  221.4 87.9 %copy-start = (f32[768,768]{1,0:T(8,128)}, f32[768,768]{1,0:T(8,128)S(1)}, u32[]{:S(2)}) copy-start(f32[768,768]{1,0:T(8,128)S(1)} %get-tuple-element.317) | copy-start | bytes 7077892
  221.4 87.8 %copy-start.34 = (f32[768]{0:T(1024)}, f32[768]{0:T(1024)S(1)}, u32[]{:S(2)}) copy-start(f32[768]{0:T(1024)S(1)} %broadcast_multiply_fusion.5) | copy-start | bytes 9220
  221.8 87.4 %copy-start.37 = (f32[768]{0:T(1024)}, f32[768]{0:T(1024)S(1)}, u32[]{:S(2)}) copy-start(f32[768]{0:T(1024)S(1)} %add_rsqrt_fusion) | copy-start | bytes 9220
  281.7 11.6 %copy-start.20 = (bf16[32,64,768]{2,1,0:T(8,128)(2,1)S(1)}, bf16[32,64,768]{2,1,0:T(8,128)(2,1)}, u32[]{:S(2)}) copy-start(bf16[32,64,768]{2,1,0:T(8,128)(2,1)} %slice.107) | copy-start | bytes 9437188
  281.7 11.6 %copy-start.28 = (bf16[3,256,768]{2,1,0:T(8,128)(2,1)S(1)}, bf16[3,256,768]{2,1,0:T(8,128)(2,1)}, u32[]{:S(2)}) copy-start(bf16[3,256,768]{2,1,0:T(8,128)(2,1)} %get-tuple-element.308) | copy-start | bytes 3538948
  281.7 20.9 %slice-start.2 = ((s8[6291456]{0:T(1024)(128)(4,1)}), s8[4194304]{0:T(1024)(128)(4,1)S(1)}, s32[]{:S(2)}) async-start(s8[6291456]{0:T(1024)(128)(4,1)} %bitcast.214), calls=%async_computation.12 | async-start | bytes 8388608
  293.3 9.3 %slice-start.3 = ((s8[6291456]{0:T(1024)(128)(4,1)}), s8[2097152]{0:T(1024)(128)(4,1)S(1)}, s32[]{:S(2)}) async-start(s8[6291456]{0:T(1024)(128)(4,1)} %bitcast.214), calls=%async_computation.13 | async-start | bytes 4194304
  302.6 6.6 copy-start.22
  302.6 6.6 copy-start.23
  302.6 6.7 copy-start.13
  317.3 4.7 copy-start.10
  322.2 5.6 copy-start.14
  353.7 5.5 copy-start.14
  385.1 5.5 copy-start.14
  418.0 95.5 %reduce-scatter.6.cloned.1.call-start = ((), (), s32[]{:S(2)}) async-start(), calls=%async_computation.7 | async-start | bytes 5898240 | tf_op jit(solution)/shard_map/reduce_scatter | solution.py:197
  418.5 400.2 %reduce-scatter.8.cloned.1.call-start = ((), (), s32[]{:S(2)}) async-start(), calls=%async_computation.8 | async-start | bytes 29196288 | tf_op jit(solution)/shard_map/reduce_scatter | solution.py:218
  418.6 5.2 copy-start.1
  418.6 5.2 copy-start.35
  418.6 5.2 copy-start.38
  437.7 14.5 %copy-start.16 = (bf16[96,8,3,256]{3,1,2,0:T(8,128)(2,1)S(1)}, bf16[96,8,3,256]{3,1,2,0:T(8,128)(2,1)}, u32[]{:S(2)}) copy-start(bf16[96,8,3,256]{3,1,2,0:T(8,128)(2,1)} %copy-done.15) | copy-start | bytes 3538948
  452.2 4.3 copy-start.21
  452.2 4.3 copy-start.29
  456.5 6.7 copy-start.33
  556.3 5.6 copy-start.45
  556.3 6.8 copy-start.9
  556.3 6.8 copy-start.19
  (28 other events, 59.1 us)
Sparse Core Ops, SparseCore 0:
  11.5 64.5 all-gather.5
  98.6 36.4 all-gather.11
  136.7 38.0 all-gather.7
  178.1 81.2 all-gather.9
  416.7 46.5 reduce-scatter.3
  465.6 47.7 reduce-scatter.5
  555.8 262.8 reduce-scatter.7
where the time goes:
time: 843 us; the launch traced here: 833 us
  waiting for transfers between devices  458 us (54%)
  matrix products  166 us (20%)
  local copies, waits for them, and re-layouts  110 us (13%)
  other arithmetic  82.5 us (10%)
  between operations  15.3 us (2%)
    reduce_scatter x1, waiting for transfers between devices, on_device(): lax.psum_scatter(block_terms(all_pairs, all_rows, model_width, lax.axis_s...  250 us
    all_gather x1, waiting for transfers between devices, attention_weights(): gathered = lax.all_gather(packed, ('dp', 'seq'), axis=0, tiled=True)  62.2 us
    reduce_scatter x1, waiting for transfers between devices, on_device(): lax.psum_scatter(grad_value_all.astype(jnp.bfloat16), 'seq', scatter_dime...  43.4 us
    all_gather x1, waiting for transfers between devices, on_device(): lax.all_gather(key_bf, 'seq', axis=1, tiled=True)  39.6 us
    all_gather x1, waiting for transfers between devices, ffn_weights(): gathered = lax.all_gather(packed, ('dp', 'seq'), axis=0, tiled=True)  37.6 us
    dot_general x4, matrix products, block_terms(): lax.dot_general(left_side, right_side, (((0,), (0,)), ((), ())), preferre...  27.8 us
    dot_general x3, matrix products, backward_slot(): jnp.einsum('qhd,khd->hqk', grad_mixed_one, value_one, preferred_element_t...  26.7 us
    reshape x2, local copies, waits for them, and re-layouts, block_terms(): term_parts.append(term_piece.reshape(blocks, -1, model_width))  22.8 us
  transfers between devices with their start and end apart: 7, of which 7 were waited for; matrix products, arithmetic and copies ran while one was open for 15% of the time, Pallas kernels for 0%

commit v1 on v0

--- a/solution.py
+++ b/solution.py
@@ -1,9 +1,450 @@
+import functools
 import jax
 import jax.numpy as jnp
 from jax import lax
+from jax.experimental import pallas as pl
+from jax.experimental.pallas import tpu as pltpu
 from jax.sharding import PartitionSpec as P
 
+MESH = pl.DeviceIdType.MESH
+
+
+def placement():
+    dp, seq = lax.axis_index("dp"), lax.axis_index("seq")
+    return dp // 2, dp % 2, seq // 2, seq % 2
+
+
+def device(outer, inner, y, core):
+    return {"dp": outer * 2 + inner, "seq": y * 2 + core}
+
+
+def slot_of(outer, inner, y, core):
+    return (outer * 2 + inner) * 4 + y * 2 + core
+
+
+def greet(n_outer, o, i, y, c):
+    barrier = pltpu.get_barrier_semaphore()
+
+    def signal(target):
+        pl.semaphore_signal(barrier, inc=1, device_id=target, device_id_type=MESH)
+
+    signal(device(o, 1 - i, y, c))
+    signal(device(o, i, 1 - y, c))
+    signal(device(o, i, y, 1 - c))
+
+    @pl.when(o > 0)
+    def _():
+        signal(device(o - 1, i, y, c))
+
+    @pl.when(o < n_outer - 1)
+    def _():
+        signal(device(o + 1, i, y, c))
+
+    pl.semaphore_wait(barrier, 3 + jnp.where(o > 0, 1, 0) + jnp.where(o < n_outer - 1, 1, 0))
+
+
+KINDS = ("up", "down", "x", "y", "da", "db", "c_own", "c_x", "c_y", "c_da", "c_db")
+
+
+class Gather:
+    def __init__(self, n_outer, ins, outs, send, recv, local):
+        self.n, self.ins, self.outs = n_outer, ins, outs
+        self.send_sems, self.recv_sems, self.local = send, recv, local
+        self.o, self.i, self.y, self.c = placement()
+
+    def piece(self, a, slot, half=None):
+        cols = self.outs[a].shape[2]
+        if half is None:
+            return self.outs[a].at[slot]
+        return self.outs[a].at[slot, :, pl.ds(half * (cols // 2), cols // 2)]
+
+    def copy(self, kind, s, a, src, dst, target):
+        k = KINDS.index(kind)
+        return pltpu.make_async_remote_copy(
+            src_ref=src, dst_ref=dst, send_sem=self.send_sems.at[k, s, a],
+            recv_sem=self.recv_sems.at[k, s, a], device_id=target, device_id_type=MESH)
+
+    def arrays(self):
+        return range(len(self.ins))
+
+    def send(self, kind, s, slot, target, half=None, own=False):
+        for a in self.arrays():
+            ref = self.piece(a, slot, half)
+            self.copy(kind, s, a, self.ins[a] if own else ref, ref, target).start()
+
+    def wait_recv(self, kind, s, slot, half=None):
+        for a in self.arrays():
+            ref = self.piece(a, slot, half)
+            self.copy(kind, s, a, ref, ref, self.core_mate()).wait_recv()
+
+    def wait_send(self, kind, s, slot, half=None):
+        for a in self.arrays():
+            ref = self.piece(a, slot, half)
+            self.copy(kind, s, a, ref, ref, self.core_mate()).wait_send()
+
+    def x_mate(self):
+        return device(self.o, 1 - self.i, self.y, self.c)
+
+    def y_mate(self):
+        return device(self.o, self.i, 1 - self.y, self.c)
+
+    def core_mate(self):
+        return device(self.o, self.i, self.y, 1 - self.c)
+
+    def spread(self, s, own=False):
+        slot = slot_of(s, self.i, self.y, self.c)
+        self.send("x", s, slot, self.x_mate(), own=own)
+        self.send("y", s, slot, self.y_mate(), own=own)
+        self.send("c_own", s, slot, self.core_mate(), own=own)
+
+    def start(self):
+        o, i, y, c = self.o, self.i, self.y, self.c
+        slot = slot_of(o, i, y, c)
+
+        @pl.when(o < self.n - 1)
+        def _():
+            self.send("up", o, slot, device(o + 1, i, y, c), own=True)
+
+        @pl.when(o > 0)
+        def _():
+            self.send("down", o, slot, device(o - 1, i, y, c), own=True)
+
+        self.spread(o, own=True)
+        for a in self.arrays():
+            pltpu.make_async_copy(self.ins[a], self.piece(a, slot), self.local.at[a]).start()
+
+    def line(self, k):
+        o, i, y, c = self.o, self.i, self.y, self.c
+
+        @pl.when(o - k >= 0)
+        def _():
+            s = o - k
+            slot = slot_of(s, i, y, c)
+            self.wait_recv("up", s, slot)
+
+            @pl.when(o < self.n - 1)
+            def _():
+                self.send("up", s, slot, device(o + 1, i, y, c))
+
+            self.spread(s)
+
+        @pl.when(o + k < self.n)
+        def _():
+            s = o + k
+            slot = slot_of(s, i, y, c)
+            self.wait_recv("down", s, slot)
+
+            @pl.when(o > 0)
+            def _():
+                self.send("down", s, slot, device(o - 1, i, y, c))
+
+            self.spread(s)
+
+    def plane(self, s):
+        i, y, c = self.i, self.y, self.c
+        from_x, from_y = slot_of(s, 1 - i, y, c), slot_of(s, i, 1 - y, c)
+        self.wait_recv("x", s, from_x)
+        self.send("da", s, from_x, self.y_mate(), half=0)
+        self.send("c_x", s, from_x, self.core_mate())
+        self.wait_recv("y", s, from_y)
+        self.send("db", s, from_y, self.x_mate(), half=1)
+        self.send("c_y", s, from_y, self.core_mate())
+
+    def far(self, s):
+        i, y, c = self.i, self.y, self.c
+        slot = slot_of(s, 1 - i, 1 - y, c)
+        self.wait_recv("da", s, slot, half=0)
+        self.send("c_da", s, slot, self.core_mate(), half=0)
+        self.wait_recv("db", s, slot, half=1)
+        self.send("c_db", s, slot, self.core_mate(), half=1)
+
+    def both(self, k, step):
+        if k == 0:
+            step(self.o)
+            return
+
+        @pl.when(self.o - k >= 0)
+        def _():
+            step(self.o - k)
+
+        @pl.when(self.o + k < self.n)
+        def _():
+            step(self.o + k)
+
+    def finish(self):
+        o, i, y, c = self.o, self.i, self.y, self.c
+
+        def close(s, carry):
+            other = 1 - c
+            self.wait_recv("c_own", s, slot_of(s, i, y, other))
+            self.wait_recv("c_x", s, slot_of(s, 1 - i, y, other))
+            self.wait_recv("c_y", s, slot_of(s, i, 1 - y, other))
+            self.wait_recv("c_da", s, slot_of(s, 1 - i, 1 - y, other), half=0)
+            self.wait_recv("c_db", s, slot_of(s, 1 - i, 1 - y, other), half=1)
+            slot = slot_of(s, i, y, c)
+            for kind in ("x", "y", "c_own", "c_x", "c_y"):
+                self.wait_send(kind, s, slot)
+            self.wait_send("da", s, slot, half=0)
+            self.wait_send("db", s, slot, half=1)
+            self.wait_send("c_da", s, slot, half=0)
+            self.wait_send("c_db", s, slot, half=1)
+
+            @pl.when((s <= o) & (o < self.n - 1))
+            def _():
+                self.wait_send("up", s, slot)
+
+            @pl.when((s >= o) & (o > 0))
+            def _():
+                self.wait_send("down", s, slot)
+
+            return carry
+
+        lax.fori_loop(0, self.n, close, 0)
+        for a in self.arrays():
+            pltpu.make_async_copy(self.ins[a], self.piece(a, slot_of(o, i, y, c)), self.local.at[a]).wait()
+
+    def stages(self):
+        todo = [lambda: self.start()]
+        for k in range(self.n):
+            if k + 1 < self.n:
+                todo.append(functools.partial(self.line, k + 1))
+            todo.append(functools.partial(self.both, k, self.plane))
+            todo.append(functools.partial(self.both, k, self.far))
+        todo.append(self.finish)
+        return todo
+
+
+def gather_scratch(n_outer, count):
+    return [
+        pltpu.SemaphoreType.DMA((len(KINDS), n_outer, count)),
+        pltpu.SemaphoreType.DMA((len(KINDS), n_outer, count)),
+        pltpu.SemaphoreType.DMA((count,)),
+    ]
+
+
+def gather_rows(shards, collective_id):
+    n_outer = lax.axis_size("dp") // 2
+    count = len(shards)
+
+    def kernel(*refs):
+        ins, outs = refs[:count], refs[count:2 * count]
+        send, recv, local = refs[2 * count:]
+        greet(n_outer, *placement())
+        for stage in Gather(n_outer, ins, outs, send, recv, local).stages():
+            stage()
+
+    devices = lax.axis_size(("dp", "seq"))
+    return pl.pallas_call(
+        kernel,
+        out_shape=[jax.ShapeDtypeStruct((devices,) + v.shape, v.dtype) for v in shards],
+        in_specs=[pl.BlockSpec(memory_space=pl.ANY)] * count,
+        out_specs=[pl.BlockSpec(memory_space=pl.ANY)] * count,
+        scratch_shapes=gather_scratch(n_outer, count),
+        compiler_params=pltpu.CompilerParams(collective_id=collective_id, has_side_effects=True),
+        name="gather_rows",
+    )(*shards)
+
 HEAD_DIM = 64
+
+RKINDS = ("da", "db", "x", "y", "up", "down")
+
+
+class Scatter:
+    def __init__(self, n_outer, ins, outs, scratch):
+        count = len(ins)
+        self.n, self.ins, self.outs, self.count = n_outer, ins, outs, count
+        groups = [scratch[g * count:(g + 1) * count] for g in range(7)]
+        self.acc, self.cbuf, self.far, self.xbuf, self.ybuf, self.upbuf, self.downbuf = groups
+        self.send_sems, self.recv_sems, self.local = scratch[7 * count:]
+        self.o, self.i, self.y, self.c = placement()
+
+    def half(self, ref, h):
+        cols = ref.shape[-1] // 2
+        return ref.at[:, pl.ds(h * cols, cols)]
+
+    def quad(self, i, y):
+        return i * 2 + y
+
+    def core_copy(self, s, a, q):
+        slot = slot_of(s, q // 2, q % 2, 1 - self.c)
+        return pltpu.make_async_remote_copy(
+            src_ref=self.ins[a].at[slot], dst_ref=self.cbuf[a].at[s, q],
+            send_sem=self.send_sems.at[len(RKINDS) + q, s, a], recv_sem=self.recv_sems.at[len(RKINDS) + q, s, a],
+            device_id=device(self.o, self.i, self.y, 1 - self.c), device_id_type=MESH)
+
+    def own_copy(self, s, a, q):
+        slot = slot_of(s, q // 2, q % 2, self.c)
+        return pltpu.make_async_copy(self.ins[a].at[slot], self.acc[a].at[s, q], self.local.at[s, a, q])
+
+    def hop(self, kind, s, a):
+        o, i, y, c = self.o, self.i, self.y, self.c
+        far, via_x, via_y, own = (self.quad(1 - i, 1 - y), self.quad(1 - i, y), self.quad(i, 1 - y), self.quad(i, y))
+        acc = self.acc[a]
+        plan = {
+            "da": lambda: (self.half(acc.at[s, far], 0), self.far[a].at[0, s], device(o, i, 1 - y, c)),
+            "db": lambda: (self.half(acc.at[s, far], 1), self.far[a].at[1, s], device(o, 1 - i, y, c)),
+            "x": lambda: (acc.at[s, via_x], self.xbuf[a].at[s], device(o, 1 - i, y, c)),
+            "y": lambda: (acc.at[s, via_y], self.ybuf[a].at[s], device(o, i, 1 - y, c)),
+            "up": lambda: (acc.at[s, own], self.upbuf[a].at[s], device(o + 1, i, y, c)),
+            "down": lambda: (acc.at[s, own], self.downbuf[a].at[s], device(o - 1, i, y, c)),
+        }
+        src, dst, target = plan[kind]()
+        k = RKINDS.index(kind)
+        return pltpu.make_async_remote_copy(
+            src_ref=src, dst_ref=dst, send_sem=self.send_sems.at[k, s, a],
+            recv_sem=self.recv_sems.at[k, s, a], device_id=target, device_id_type=MESH)
+
+    def target_slice(self, t):
+        return jnp.where(t % 2 == 0, self.n - 1 - t // 2, t // 2)
+
+    def begin(self, t, carry):
+        s = self.target_slice(t)
+        for a in range(self.count):
+            for j in range(4):
+                q = 3 - j
+                self.core_copy(s, a, q).start()
+                self.own_copy(s, a, q).start()
+        return carry
+
+    def pair(self, s, a):
+        for q in range(4):
+            self.core_copy(s, a, q).wait_recv()
+            self.own_copy(s, a, q).wait()
+            self.acc[a][s, q] = (self.acc[a][s, q].astype(jnp.float32)
+                                 + self.cbuf[a][s, q].astype(jnp.float32)).astype(jnp.bfloat16)
+
+    def first(self, s):
+        for a in range(self.count):
+            self.pair(s, a)
+            self.hop("da", s, a).start()
+            self.hop("db", s, a).start()
+
+    def second(self, s):
+        for a in range(self.count):
+            cols = self.acc[a].shape[-1] // 2
+            for h, kind, q in ((0, "da", self.quad(1 - self.i, self.y)), (1, "db", self.quad(self.i, 1 - self.y))):
+                self.hop(kind, s, a).wait_recv()
+                window = pl.ds(h * cols, cols)
+                self.acc[a][s, q, :, window] = (
+                    self.acc[a][s, q, :, window].astype(jnp.float32)
+                    + self.far[a][h, s].astype(jnp.float32)).astype(jnp.bfloat16)
+                self.hop("x" if h == 0 else "y", s, a).start()
+
+    def third(self, s):
+        o, q = self.o, self.quad(self.i, self.y)
+        for a in range(self.count):
+            self.hop("x", s, a).wait_recv()
+            self.hop("y", s, a).wait_recv()
+            total = (self.acc[a][s, q].astype(jnp.float32) + self.xbuf[a][s].astype(jnp.float32)
+                     + self.ybuf[a][s].astype(jnp.float32))
+
+            @pl.when(s != o)
+            def _():
+                self.acc[a][s, q] = total.astype(jnp.bfloat16)
+
+            @pl.when(s == o)
+            def _():
+                self.outs[a][...] = total
+
+        for a in range(self.count):
+            for kind, ahead, has_before, buf in (
+                ("up", s > o, o > 0, self.upbuf), ("down", s < o, o < self.n - 1, self.downbuf)):
+
+                @pl.when(ahead)
+                def _(kind=kind, has_before=has_before, buf=buf, a=a):
+                    @pl.when(has_before)
+                    def _():
+                        self.hop(kind, s, a).wait_recv()
+                        self.acc[a][s, q] = (self.acc[a][s, q].astype(jnp.float32)
+                                             + buf[a][s].astype(jnp.float32)).astype(jnp.bfloat16)
+
+                    self.hop(kind, s, a).start()
+
+    def step(self, t, carry):
+        n = self.n
+
+        @pl.when(t < n)
+        def _():
+            self.first(self.target_slice(t))
+
+        @pl.when((t >= 1) & (t < n + 1))
+        def _():
+            self.second(self.target_slice(t - 1))
+
+        @pl.when(t >= 2)
+        def _():
+            self.third(self.target_slice(t - 2))
+
+        return carry
+
+    def finish(self):
+        o = self.o
+        for a in range(self.count):
+            for kind, there, buf in (("up", o > 0, self.upbuf), ("down", o < self.n - 1, self.downbuf)):
+
+                @pl.when(there)
+                def _(kind=kind, buf=buf, a=a):
+                    self.hop(kind, o, a).wait_recv()
+                    self.outs[a][...] += buf[a][o].astype(jnp.float32)
+
+        def close(s, carry):
+            for a in range(self.count):
+                for q in range(4):
+                    self.core_copy(s, a, q).wait_send()
+                for kind in ("da", "db", "x", "y"):
+                    self.hop(kind, s, a).wait_send()
+
+                @pl.when(s > o)
+                def _(a=a):
+                    self.hop("up", s, a).wait_send()
+
+                @pl.when(s < o)
+                def _(a=a):
+                    self.hop("down", s, a).wait_send()
+
+            return carry
+
+        lax.fori_loop(0, self.n, close, 0)
+
+    def run(self):
+        lax.fori_loop(0, self.n, self.begin, 0)
+        lax.fori_loop(0, self.n + 2, self.step, 0)
+        self.finish()
+
+
+def scatter_scratch(n, shapes):
+    bf = jnp.bfloat16
+    scratch = [pltpu.VMEM((n, 4) + s, bf) for s in shapes]
+    scratch += [pltpu.VMEM((n, 4) + s, bf) for s in shapes]
+    scratch += [pltpu.VMEM((2, n, s[0], s[1] // 2), bf) for s in shapes]
+    for _ in range(4):
+        scratch += [pltpu.VMEM((n,) + s, bf) for s in shapes]
+    count = len(shapes)
+    scratch += [pltpu.SemaphoreType.DMA((len(RKINDS) + 4, n, count)) for _ in range(2)]
+    scratch += [pltpu.SemaphoreType.DMA((n, count, 4))]
+    return scratch
+
+
+def scatter_rows(blocks, collective_id):
+    n_outer = lax.axis_size("dp") // 2
+    count = len(blocks)
+    shapes = [b.shape[1:] for b in blocks]
+
+    def kernel(*refs):
+        ins, outs, scratch = refs[:count], refs[count:2 * count], refs[2 * count:]
+        work = Scatter(n_outer, ins, outs, scratch)
+        greet(n_outer, *placement())
+        work.run()
+
+    return pl.pallas_call(
+        kernel,
+        out_shape=[jax.ShapeDtypeStruct(s, jnp.float32) for s in shapes],
+        in_specs=[pl.BlockSpec(memory_space=pl.ANY)] * count,
+        out_specs=[pl.BlockSpec(memory_space=pltpu.VMEM)] * count,
+        scratch_shapes=scatter_scratch(n_outer, shapes),
+        compiler_params=pltpu.CompilerParams(collective_id=collective_id, has_side_effects=True, vmem_limit_bytes=56 << 20),
+        name="scatter_rows",
+    )(*blocks)
 
 
 def norm_rows(values):
@@ -46,41 +487,16 @@
     )
 
 
-def attention_weights(w_qkv, w_att_out):
-    model_width = w_att_out.shape[1]
-    packed = jnp.concatenate([w_qkv.reshape(-1, model_width), w_att_out], 0)
-    gathered = lax.all_gather(packed, ("dp", "seq"), axis=0, tiled=True)
-    devices = gathered.shape[0] // packed.shape[0]
-    gathered = gathered.reshape(devices, packed.shape[0], model_width)
-    split_rows = w_qkv.shape[0] * w_qkv.shape[1] // model_width
-    return (
-        gathered[:, :split_rows].reshape(-1, w_qkv.shape[1]),
-        gathered[:, split_rows:].reshape(-1, model_width),
-    )
-
-
-def ffn_weights(w_ffin, w_ffout):
-    model_width = w_ffout.shape[1]
-    packed = jnp.concatenate([w_ffin.reshape(-1, model_width), w_ffout], 0)
-    gathered = lax.all_gather(packed, ("dp", "seq"), axis=0, tiled=True)
-    devices = gathered.shape[0] // packed.shape[0]
-    gathered = gathered.reshape(devices, packed.shape[0], model_width)
-    split_rows = w_ffin.shape[0] * w_ffin.shape[1] // model_width
-    return (
-        gathered[:, :split_rows].reshape(-1, w_ffin.shape[1]),
-        gathered[:, split_rows:].reshape(-1, model_width),
-    )
-
-
-def block_terms(term_pairs, packed_rows, model_width, row_span):
-    blocks = row_span // packed_rows
-    term_parts = []
-    for left_side, right_side, share_rows in term_pairs:
-        term_piece = lax.dot_general(
-            left_side, right_side, (((0,), (0,)), ((), ())), preferred_element_type=jnp.float32
-        )
-        term_parts.append(term_piece.reshape(blocks, -1, model_width))
-    return jnp.concatenate(term_parts, 1).reshape(row_span, model_width)
+def gather_weights(first, second, collective_id):
+    one, two = gather_rows((first, second), collective_id)
+    return one.reshape(-1, first.shape[1]), two.reshape(-1, second.shape[1])
+
+
+def weight_term(left_side, right_side):
+    term = lax.dot_general(
+        left_side, right_side, (((0,), (0,)), ((), ())), preferred_element_type=jnp.float32
+    )
+    return term.astype(jnp.bfloat16).reshape(lax.axis_size(("dp", "seq")), -1, term.shape[1])
 
 
 def on_device(tokens, lengths, w_qkv, w_att_out, w_ffin, w_ffout, cotangent):
@@ -143,7 +559,7 @@
     inputs = tokens.astype(jnp.float32).reshape(row_count, model_width)
     normed_one, inverse_one = norm_rows(inputs)
     normed_one_bf = normed_one.astype(jnp.bfloat16)
-    qkv_full, att_out_full = attention_weights(w_qkv, w_att_out)
+    qkv_full, att_out_full = gather_weights(w_qkv, w_att_out, 1)
     project = jnp.dot(normed_one_bf, qkv_full, preferred_element_type=jnp.float32)
     project = project.reshape(slot_count, local_len, 3, head_count, HEAD_DIM)
     query_bf = rotate(project[:, :, 0], cosine, sine_table).astype(jnp.bfloat16)
@@ -158,7 +574,7 @@
     hidden_state = inputs + jnp.dot(mixed_bf, att_out_full, preferred_element_type=jnp.float32)
     normed_two, inverse_two = norm_rows(hidden_state)
     normed_two_bf = normed_two.astype(jnp.bfloat16)
-    ffin_full, ffout_full = ffn_weights(w_ffin, w_ffout)
+    ffin_full, ffout_full = gather_weights(w_ffin, w_ffout, 2)
     gate_up = jnp.dot(normed_two_bf, ffin_full, preferred_element_type=jnp.float32)
     half_units = gate_up.shape[1] // 2
     up_part = gate_up[:, :half_units]
@@ -169,21 +585,15 @@
     block_output = (valid_rows * (hidden_state + branch).reshape(tokens.shape)).astype(jnp.bfloat16)
     grad_out = (valid_rows * cotangent.astype(jnp.float32)).reshape(row_count, model_width)
     grad_out_bf = grad_out.astype(jnp.bfloat16)
-    ffin_back, ffout_back = ffn_weights(w_ffin, w_ffout)
+    ffin_back, ffout_back = ffin_full, ffout_full
     grad_act = contract_last(grad_out_bf, ffout_back)
     grad_up = grad_act * gate_part * gate_sigmoid
     grad_gate = grad_act * up_part * gate_sigmoid * (1.0 + gate_part * (1.0 - gate_sigmoid))
     grad_gate_up_bf = jnp.concatenate([grad_up, grad_gate], 1).astype(jnp.bfloat16)
-    ffn_pairs = (
-        (normed_two_bf, grad_gate_up_bf, w_ffin.shape[0]),
-        (activated_bf, grad_out_bf, w_ffout.shape[0]),
-    )
-    ffn_rows = w_ffin.shape[0] * w_ffin.shape[1] // model_width + w_ffout.shape[0]
-    att_rows = w_qkv.shape[0] * w_qkv.shape[1] // model_width + w_att_out.shape[0]
     grad_normed_two = contract_last(grad_gate_up_bf, ffin_back)
     grad_hidden = grad_out + norm_back(grad_normed_two, normed_two, inverse_two)
     grad_hidden_bf = grad_hidden.astype(jnp.bfloat16)
-    qkv_back, att_out_back = attention_weights(w_qkv, w_att_out)
+    qkv_back, att_out_back = qkv_full, att_out_full
     grad_mixed_bf = contract_last(grad_hidden_bf, att_out_back).astype(jnp.bfloat16)
     grad_mixed_bf = grad_mixed_bf.reshape(slot_count, local_len, head_count, HEAD_DIM)
     key_use, value_use = (key_all, value_all)
@@ -209,26 +619,15 @@
     grad_project_bf = grad_project_bf.reshape(row_count, 3 * model_width).astype(jnp.bfloat16)
     grad_normed_one = contract_last(grad_project_bf, qkv_back)
     grad_tokens = grad_hidden + norm_back(grad_normed_one, normed_one, inverse_one)
-    att_pairs = (
-        (normed_one_bf, grad_project_bf, w_qkv.shape[0]),
-        (mixed_bf, grad_hidden_bf, w_att_out.shape[0]),
-    )
-    all_pairs = att_pairs + ffn_pairs
-    all_rows = att_rows + ffn_rows
-    whole_block = lax.psum_scatter(
-        block_terms(all_pairs, all_rows, model_width, lax.axis_size(("dp", "seq")) * all_rows),
-        ("dp", "seq"),
-        scatter_dimension=0,
-        tiled=True,
-    )
-    att_block = whole_block[:att_rows]
-    ffn_block = whole_block[att_rows:]
-    qkv_rows = att_rows - w_att_out.shape[0]
-    ffin_rows = ffn_rows - w_ffout.shape[0]
-    grad_qkv = att_block[:qkv_rows].reshape(w_qkv.shape)
-    grad_att_out = att_block[qkv_rows:]
-    grad_ffin = ffn_block[:ffin_rows].reshape(w_ffin.shape)
-    grad_ffout = ffn_block[ffin_rows:]
+    grad_qkv, grad_att_out, grad_ffin, grad_ffout = scatter_rows(
+        (
+            weight_term(normed_one_bf, grad_project_bf),
+            weight_term(mixed_bf, grad_hidden_bf),
+            weight_term(normed_two_bf, grad_gate_up_bf),
+            weight_term(activated_bf, grad_out_bf),
+        ),
+        3,
+    )
     return (
         block_output,
         grad_tokens.reshape(tokens.shape),

time: 843 us -> 571 us (0.68)
  waiting for transfers between devices: 458 us -> 85.4 us
  Pallas kernels: 0 us -> 191 us
  local copies, waits for them, and re-layouts: 110 us -> 51 us
  other arithmetic: 82.5 us -> 58.6 us
    reduce_scatter x1 -> x0, waiting for transfers between devices: 250 us -> none  [on_device(): lax.psum_scatter(block_terms(all_pairs, all_rows, model_width, lax.axis_s...]
    pallas_call x0 -> x3, Pallas kernels: none -> 191 us  [the longest x2 106 us: gather_rows(): pl.pallas_call(kernel, out_shape=[jax.ShapeDtypeStruct((devices,) + v.sha...]
    all_gather x2 -> x0, waiting for transfers between devices: 99.8 us -> none  [the longest x1 62.2 us: attention_weights(): gathered = lax.all_gather(packed, ('dp', 'seq'), axis=0, tiled=True)]
    reshape x8 -> x0, local copies, waits for them, and re-layouts: 43.1 us -> none  [the longest x2 22.8 us: block_terms(): term_parts.append(term_piece.reshape(blocks, -1, model_width))]
    all_gather x1, waiting for transfers between devices: 22.7 us -> 0.01 us  [on_device(): lax.all_gather(value_bf, 'seq', axis=1, tiled=True)]
    concatenate x3 -> x0, other arithmetic: 22.6 us -> none  [the longest x1 20.4 us: block_terms(): return jnp.concatenate(term_parts, 1).reshape(row_span, model_width)]
    slice x8 -> x0, local copies, waits for them, and re-layouts: 21.4 us -> none  [the longest x1 6.11 us: ffn_weights(): gathered[:, :split_rows].reshape(-1, w_ffin.shape[1])]
    all_gather x1, waiting for transfers between devices: 39.6 us -> 18.9 us  [on_device(): lax.all_gather(key_bf, 'seq', axis=1, tiled=True)]
  transfers between devices with their start and end apart: 7 -> 4, of which waited for: 7 -> 3; matrix products, arithmetic and copies ran while one was open for 15% -> 6% of each run, Pallas kernels for 0% -> 14%
where the time goes in v1:
time: 571 us; the launch traced here: 563 us
  Pallas kernels  191 us (33%)
  matrix products  161 us (28%)
  waiting for transfers between devices  85.4 us (15%)
  other arithmetic  58.6 us (10%)
  local copies, waits for them, and re-layouts  51 us (9%)
  between operations  14.8 us (3%)
    pallas_call x2, Pallas kernels, gather_rows(): pl.pallas_call(kernel, out_shape=[jax.ShapeDtypeStruct((devices,) + v.sha...  106 us
    pallas_call x1, Pallas kernels, scatter_rows(): pl.pallas_call(kernel, out_shape=[jax.ShapeDtypeStruct(s, jnp.float32) fo...  85.2 us
    reduce_scatter x1, waiting for transfers between devices, on_device(): lax.psum_scatter(grad_value_all.astype(jnp.bfloat16), 'seq', scatter_dime...  43.4 us
    dot_general x3, matrix products, backward_slot(): jnp.einsum('qhd,khd->hqk', grad_mixed_one, value_one, preferred_element_t...  30.2 us
    unnamed x103, local copies, waits for them, and re-layouts  26.1 us
    dot_general x4, matrix products, contract_last(): lax.dot_general(left_side, right_side, (((1,), (1,)), ((), ())), preferre...  24.8 us
    reduce_scatter x1, waiting for transfers between devices, on_device(): lax.psum_scatter(grad_key_all.astype(jnp.bfloat16), 'seq', scatter_dimens...  22.6 us
    dot_general x6, matrix products, masked_scores(): jnp.einsum('qhd,khd->hqk', query_one, key_one, preferred_element_type=jnp...  21.3 us
  transfers between devices with their start and end apart: 4, of which 3 were waited for; matrix products, arithmetic and copies ran while one was open for 6% of the time, Pallas kernels for 14%

profile of v1, /device:TPU:10, one launch (start us, length us, event | category | flops | bytes accessed | tf_op | source)
XLA Modules:
  0.0 562.5 jit_solution(6558926654069581858)
XLA Ops:
  11.5 29.7 %gather_rows.2 = (bf16[32,24,2304]{2,1,0:T(8,128)(2,1)}, bf16[32,24,768]{2,1,0:T(8,128)(2,1)}) custom-call(bf16[24,2304]{1,0:T(8,128)(2,1)} %refs_0_.2, bf16[24,768]{1,0:T(8,128)(2,1)} %refs_1_.2), custom_call_target="tpu_custom_call" | custom-call | tf_op jit(solution)/shard_map/gather_rows/pallas_call | solution.py:237
  41.2 5.8 %copy.16 = bf16[2304,768]{1,0:T(8,128)(2,1)} copy(bf16[2304,768]{0,1:T(8,128)(2,1)} %bitcast.209) | data formatting | bytes 7077888 | tf_op jit(solution)/shard_map/dot_general | solution.py:563
  47.0 5.0 fusion.94
  63.9 76.1 %gather_rows.3 = (bf16[32,24,4096]{2,1,0:T(8,128)(2,1)}, bf16[32,64,768]{2,1,0:T(8,128)(2,1)}) custom-call(bf16[24,4096]{1,0:T(8,128)(2,1)} %refs_0_.3, bf16[64,768]{1,0:T(8,128)(2,1)} %refs_1_.3), custom_call_target="tpu_custom_call" | custom-call | tf_op jit(solution)/shard_map/gather_rows/pallas_call | solution.py:237
  142.8 18.9 %all-gather.4.cloned.1.call-done = bf16[3,1024,12,64]{1,3,2,0:T(8,128)(2,1)} async-done(((bf16[3,256,12,64]{1,3,2,0:T(8,128)(2,1)}), bf16[3,1024,12,64]{1,3,2,0:T(8,128)(2,1)}) %all-gather.4.cloned.1.call-update) | async-done | bytes 4718608 | tf_op jit(solution)/shard_map/all_gather | solution.py:569
  161.7 45.6 %while.30 = (s32[]{:T(128)}, bf16[3,256,12,64]{1,3,2,0:T(8,128)(2,1)}, f32[3,12,256,1]{2,1,3,0:T(8,128)}, bf16[3,1024,12,64]{1,3,2,0:T(8,128)(2,1)}, s32[3]{0:T(...) while((s32[]{:T(128)}, ...), condition=%wide.region_5.6_spmd.clone.clone, body=%wide.region_2.5_spmd.clone.clone.sunk | while | flops 843774208 | bytes 42838140 | solution.py:572
  163.2 3.7 fusion.147
  170.6 5.7 %fusion.149 = bf16[3,256,12,64]{1,3,2,0:T(8,128)(2,1)} fusion(bf16[3,256,12,64]{1,3,2,0:T(8,128)(2,1)} %get-tuple-element.474, s32[]{:T(128)S(6)} %copy.36, f32[12,256,1024]{2,1,0:T(8,128)S(1)} %get-tuple-element.449, f32[12,256]{1,0:T(8,128)S(1)} %fusion.148, f32[12,256]{1,0:T(8,128)S(1)} %get-tuple-element.450, ...), kind=kOutput, calls=%fused_computation.17.clone.1 | convolution fusion | flops 418578432 | bytes 14836736 | tf_op jit(solution)/shard_map/while/body/eval_jaxpr/hqk,khd->qhd/dot_general | solution.py:528
  178.4 3.7 fusion.147
  185.8 5.7 %fusion.149 = bf16[3,256,12,64]{1,3,2,0:T(8,128)(2,1)} fusion(bf16[3,256,12,64]{1,3,2,0:T(8,128)(2,1)} %get-tuple-element.474, s32[]{:T(128)S(6)} %copy.36, f32[12,256,1024]{2,1,0:T(8,128)S(1)} %get-tuple-element.449, f32[12,256]{1,0:T(8,128)S(1)} %fusion.148, f32[12,256]{1,0:T(8,128)S(1)} %get-tuple-element.450, ...), kind=kOutput, calls=%fused_computation.17.clone.1 | convolution fusion | flops 418578432 | bytes 14836736 | tf_op jit(solution)/shard_map/while/body/eval_jaxpr/hqk,khd->qhd/dot_general | solution.py:528
  193.6 3.7 fusion.147
  201.0 5.7 %fusion.149 = bf16[3,256,12,64]{1,3,2,0:T(8,128)(2,1)} fusion(bf16[3,256,12,64]{1,3,2,0:T(8,128)(2,1)} %get-tuple-element.474, s32[]{:T(128)S(6)} %copy.36, f32[12,256,1024]{2,1,0:T(8,128)S(1)} %get-tuple-element.449, f32[12,256]{1,0:T(8,128)S(1)} %fusion.148, f32[12,256]{1,0:T(8,128)S(1)} %get-tuple-element.450, ...), kind=kOutput, calls=%fused_computation.17.clone.1 | convolution fusion | flops 418578432 | bytes 14836736 | tf_op jit(solution)/shard_map/while/body/eval_jaxpr/hqk,khd->qhd/dot_general | solution.py:528
  214.1 8.1 %fusion.103 = f32[768,4096]{1,0:T(8,128)} fusion(bf16[768,4096]{1,0:T(8,128)(2,1)S(1)} %bitcast.225, f32[768,768]{1,0:T(8,128)S(1)} %get-tuple-element.333, f32[768]{0:T(1024)S(1)} %add_rsqrt_fusion, f32[768]{0:T(1024)S(1)} %broadcast_multiply_fusion.5), kind=kOutput, calls=%fused_computation.150 | convolution fusion | flops 4833607680 | bytes 21239808 | tf_op jit(solution)/shard_map/dot_general | solution.py:578
  222.2 10.5 %multiply_convert_fusion.2 = (bf16[768,2048]{1,0:T(8,128)(2,1)}, bf16[768,2048]{1,0:T(8,128)(2,1)}, bf16[768,2048]{1,0:T(8,128)(2,1)}) fusion(f32[768,4096]{1,0:T(8,128)} %fusion.103, bf16[768,768]{1,0:T(8,128)(2,1)S(1)} %bitcast.222, bf16[2048,768]{1,0:T(8,128)(2,1)S(1)} %bitcast.228), kind=kOutput, calls=%fused_computation.72 | convolution fusion | flops 2441084928 | bytes 26345472 | tf_op jit(solution)/shard_map/dot_general | solution.py:485
  232.8 7.7 %fusion.106 = (f32[768]{0:T(1024)S(1)}, f32[768]{0:T(1024)S(1)}, f32[768,768]{1,0:T(8,128)S(1)}) fusion(f32[768]{0:T(1024)S(1)} %add_rsqrt_fusion, f32[768,768]{1,0:T(8,128)S(1)} %get-tuple-element.333, f32[768]{0:T(1024)S(1)} %broadcast_multiply_fusion.5, bf16[768,4096]{1,0:T(8,128)(2,1)S(1)} %bitcast.226, bf16[768,2048]{1,0:T(8,128)(2,1)} %get-tuple-element.310, ...), kind=kOutput, calls=%fused_computation.152 | convolution fusion | flops 4847368192 | bytes 17313792 | tf_op jit(solution)/shard_map/dot_general | solution.py:485
  247.2 4.7 copy.20
  251.9 96.2 %while.31 = (s32[]{:T(128)}, f32[3,256,12,64]{1,3,2,0:T(8,128)S(1)}, bf16[3,1024,12,64]{1,3,2,0:T(8,128)(2,1)}, bf16[3,1024,12,64]{1,3,2,0:T(8,128)(2,1)}, bf16[...) while((s32[]{:T(128)}, ...), condition=%wide.region_12.13_spmd.clone.clone, body=%wide.region_10.12_spmd.clone.clone.sunk | while | flops 2061957376 | bytes 146642192 | solution.py:600
  261.4 10.1 %multiply_reduce_fusion.4 = (f32[12,256]{1,0:T(8,128)S(1)}, f32[12,256,1024]{2,1,0:T(8,128)}) fusion(f32[12,256,1024]{2,1,0:T(8,128)S(1)} %fusion.158, f32[12,256]{1,0:T(8,128)S(1)} %dynamic-slice_bitcast_fusion.2, pred[256,1024]{1,0:T(8,128)(4,1)S(1)} %fusion.159, bf16[3,1024,12,64]{1,3,2,0:T(8,128)(2,1)} %get-tuple-element.524, s32[]{:T(128)S(6)} %copy.46, ...), kind=kOutput, calls=%fused_computation.30.clone.1 | convolution fusion | flops 418378752 | bytes 27423744 | tf_op jit(solution)/shard_map/while/body/eval_jaxpr/qhd,khd->hqk/dot_general | solution.py:537
  271.5 6.7 %multiply_convert_fusion.6 = bf16[12,256,1024]{2,1,0:T(8,128)(2,1)S(1)} fusion(f32[12,256,1024]{2,1,0:T(8,128)} %get-tuple-element.462, f32[12,256,1024]{2,1,0:T(8,128)S(1)} %fusion.158, f32[12,256]{1,0:T(8,128)S(1)} %get-tuple-element.463, f32[12,256]{1,0:T(8,128)S(1)} %dynamic-slice_bitcast_fusion.2, pred[256,1024]{1,0:T(8,128)(4,1)S(1)} %fusion.159), kind=kLoop, calls=%fused_computation.29.clone.1 | loop fusion | flops 18874368 | bytes 31744000 | tf_op jit(solution)/shard_map/while/body/eval_jaxpr/convert_element_type | solution.py:543
  293.4 10.1 %multiply_reduce_fusion.4 = (f32[12,256]{1,0:T(8,128)S(1)}, f32[12,256,1024]{2,1,0:T(8,128)}) fusion(f32[12,256,1024]{2,1,0:T(8,128)S(1)} %fusion.158, f32[12,256]{1,0:T(8,128)S(1)} %dynamic-slice_bitcast_fusion.2, pred[256,1024]{1,0:T(8,128)(4,1)S(1)} %fusion.159, bf16[3,1024,12,64]{1,3,2,0:T(8,128)(2,1)} %get-tuple-element.524, s32[]{:T(128)S(6)} %copy.46, ...), kind=kOutput, calls=%fused_computation.30.clone.1 | convolution fusion | flops 418378752 | bytes 27423744 | tf_op jit(solution)/shard_map/while/body/eval_jaxpr/qhd,khd->hqk/dot_general | solution.py:537
  303.5 6.7 %multiply_convert_fusion.6 = bf16[12,256,1024]{2,1,0:T(8,128)(2,1)S(1)} fusion(f32[12,256,1024]{2,1,0:T(8,128)} %get-tuple-element.462, f32[12,256,1024]{2,1,0:T(8,128)S(1)} %fusion.158, f32[12,256]{1,0:T(8,128)S(1)} %get-tuple-element.463, f32[12,256]{1,0:T(8,128)S(1)} %dynamic-slice_bitcast_fusion.2, pred[256,1024]{1,0:T(8,128)(4,1)S(1)} %fusion.159), kind=kLoop, calls=%fused_computation.29.clone.1 | loop fusion | flops 18874368 | bytes 31744000 | tf_op jit(solution)/shard_map/while/body/eval_jaxpr/convert_element_type | solution.py:543
  321.8 3.7 bitcast_dynamic-update-slice_fusion.8
  325.5 10.1 %multiply_reduce_fusion.4 = (f32[12,256]{1,0:T(8,128)S(1)}, f32[12,256,1024]{2,1,0:T(8,128)}) fusion(f32[12,256,1024]{2,1,0:T(8,128)S(1)} %fusion.158, f32[12,256]{1,0:T(8,128)S(1)} %dynamic-slice_bitcast_fusion.2, pred[256,1024]{1,0:T(8,128)(4,1)S(1)} %fusion.159, bf16[3,1024,12,64]{1,3,2,0:T(8,128)(2,1)} %get-tuple-element.524, s32[]{:T(128)S(6)} %copy.46, ...), kind=kOutput, calls=%fused_computation.30.clone.1 | convolution fusion | flops 418378752 | bytes 27423744 | tf_op jit(solution)/shard_map/while/body/eval_jaxpr/qhd,khd->hqk/dot_general | solution.py:537
  335.5 6.7 %multiply_convert_fusion.6 = bf16[12,256,1024]{2,1,0:T(8,128)(2,1)S(1)} fusion(f32[12,256,1024]{2,1,0:T(8,128)} %get-tuple-element.462, f32[12,256,1024]{2,1,0:T(8,128)S(1)} %fusion.158, f32[12,256]{1,0:T(8,128)S(1)} %get-tuple-element.463, f32[12,256]{1,0:T(8,128)S(1)} %dynamic-slice_bitcast_fusion.2, pred[256,1024]{1,0:T(8,128)(4,1)S(1)} %fusion.159), kind=kLoop, calls=%fused_computation.29.clone.1 | loop fusion | flops 18874368 | bytes 31744000 | tf_op jit(solution)/shard_map/while/body/eval_jaxpr/convert_element_type | solution.py:543
  352.9 5.5 convolution_add_fusion
  363.7 4.3 convolution_convert_fusion.2
  368.0 7.9 %convolution_convert_fusion = bf16[768,4096]{1,0:T(8,128)(2,1)} fusion(bf16[768,2048]{1,0:T(8,128)(2,1)} %get-tuple-element.310, bf16[768,2048]{1,0:T(8,128)(2,1)S(1)} %copy-done.45, f32[768,768]{1,0:T(8,128)S(1)} %copy-done.6, f32[768]{0:T(1024)S(1)} %copy-done.40, f32[768]{0:T(1024)S(1)} %copy-done.34), kind=kOutput, calls=%fused_computation.69 | convolution fusion | flops 4849336320 | bytes 14948352 | tf_op jit(solution)/shard_map/dot_general | solution.py:496
  375.8 22.6 %reduce-scatter.3.cloned.1.call-done = bf16[3,256,12,64]{1,3,2,0:T(8,128)(2,1)} async-done(((bf16[3,1024,12,64]{1,3,2,0:T(8,128)(2,1)}), bf16[3,256,12,64]{1,3,2,0:T(8,128)(2,1)}) %reduce-scatter.3.cloned.1.call-update) | async-done | bytes 1179664 | tf_op jit(solution)/shard_map/reduce_scatter | solution.py:604
  405.2 43.4 %reduce-scatter.5.cloned.1.call-done = bf16[3,256,12,64]{1,3,2,0:T(8,128)(2,1)} async-done(((bf16[3,1024,12,64]{1,3,2,0:T(8,128)(2,1)}), bf16[3,256,12,64]{1,3,2,0:T(8,128)(2,1)}) %reduce-scatter.5.cloned.1.call-update) | async-done | bytes 1179664 | tf_op jit(solution)/shard_map/reduce_scatter | solution.py:607
  455.1 4.8 convolution_convert_fusion.1
  459.9 85.2 %scatter_rows.1 = (f32[24,2304]{1,0:T(8,128)}, f32[24,768]{1,0:T(8,128)}, f32[24,4096]{1,0:T(8,128)}, f32[64,768]{1,0:T(8,128)}) custom-call(bf16[32,24,2304]{2,1,0:T(8,128)(2,1)} %bitcast.208, bf16[32,24,768]{2,1,0:T(8,128)(2,1)} %bitcast.217, bf16[32,24,4096]{2,1,0:T(8,128)(2,1)} %bitcast.204, bf16[32,64,768]{2,1,0:T(8,128)(2,1)} %bitcast.214), custom_call_target="tpu_custom_call" | custom-call | tf_op jit(solution)/shard_map/scatter_rows/pallas_call | solution.py:439
  545.1 5.5 fusion.105
  (229 shorter events, 119.3 us)
Async XLA Ops:
  7.2 4.0 copy-start.2
  7.2 135.6 %all-gather.6.cloned.1.call-start = ((), (), s32[]{:S(2)}) async-start(), calls=%async_computation.5 | async-start | bytes 5898240 | tf_op jit(solution)/shard_map/all_gather | solution.py:570
  11.5 35.5 %copy-start.17 = (bf16[3,256,768]{2,1,0:T(8,128)(2,1)}, bf16[3,256,768]{2,1,0:T(8,128)(2,1)S(1)}, u32[]{:S(2)}) copy-start(bf16[3,256,768]{2,1,0:T(8,128)(2,1)S(1)} %fusion.83) | copy-start | bytes 3538948
  56.1 105.6 %all-gather.4.cloned.1.call-start = ((), (), s32[]{:S(2)}) async-start(), calls=%async_computation.2 | async-start | bytes 5898240 | tf_op jit(solution)/shard_map/all_gather | solution.py:569
  56.4 3.7 copy-start.23
  56.4 3.7 copy-start.25
  56.4 3.7 slice-start
  61.5 78.5 %copy-start.41 = (s32[3]{0:T(128)S(1)}, s32[3]{0:T(128)}, u32[]{:S(2)}) copy-start(s32[3]{0:T(128)} %param.12) | copy-start | bytes 40
  61.5 79.2 %copy-start.19 = (bf16[3,256,768]{2,1,0:T(8,128)(2,1)S(1)}, bf16[3,256,768]{2,1,0:T(8,128)(2,1)}, u32[]{:S(2)}) copy-start(bf16[3,256,768]{2,1,0:T(8,128)(2,1)} %param.17) | copy-start | bytes 3538948
  63.8 334.6 %reduce-scatter.3.cloned.1.call-start = ((), (), s32[]{:S(2)}) async-start(), calls=%async_computation.3 | async-start | bytes 5898240 | tf_op jit(solution)/shard_map/reduce_scatter | solution.py:604
  210.0 4.1 slice-start.5
  211.3 29.2 %copy-start.5 = (f32[768,768]{1,0:T(8,128)}, f32[768,768]{1,0:T(8,128)S(1)}, u32[]{:S(2)}) copy-start(f32[768,768]{1,0:T(8,128)S(1)} %get-tuple-element.333) | copy-start | bytes 7077892
  211.3 29.2 %copy-start.33 = (f32[768]{0:T(1024)}, f32[768]{0:T(1024)S(1)}, u32[]{:S(2)}) copy-start(f32[768]{0:T(1024)S(1)} %broadcast_multiply_fusion.5) | copy-start | bytes 9220
  211.8 28.7 %copy-start.39 = (f32[768]{0:T(1024)}, f32[768]{0:T(1024)S(1)}, u32[]{:S(2)}) copy-start(f32[768]{0:T(1024)S(1)} %add_rsqrt_fusion) | copy-start | bytes 9220
  214.1 8.1 %copy-start.22 = (bf16[3,256,768]{2,1,0:T(8,128)(2,1)S(1)}, bf16[3,256,768]{2,1,0:T(8,128)(2,1)}, u32[]{:S(2)}) copy-start(bf16[3,256,768]{2,1,0:T(8,128)(2,1)} %get-tuple-element.324) | copy-start | bytes 3538948
  214.1 8.1 %copy-start.42 = (bf16[32,64,768]{2,1,0:T(8,128)(2,1)S(1)}, bf16[32,64,768]{2,1,0:T(8,128)(2,1)}, u32[]{:S(2)}) copy-start(bf16[32,64,768]{2,1,0:T(8,128)(2,1)} %get-tuple-element.136) | copy-start | bytes 9437188
  232.8 7.7 %copy-start = (f32[3,256,768]{2,1,0:T(8,128)S(1)}, f32[3,256,768]{2,1,0:T(8,128)}, u32[]{:S(2)}) copy-start(f32[3,256,768]{2,1,0:T(8,128)} %get-tuple-element.325) | copy-start | bytes 7077892
  247.2 4.7 copy-start.9
  261.4 10.1 %copy-start.13 = (bf16[3,1024,12,64]{1,3,2,0:T(8,128)(2,1)}, bf16[3,1024,12,64]{1,3,2,0:T(8,128)(2,1)S(1)}, u32[]{:S(2)}) copy-start(bf16[3,1024,12,64]{1,3,2,0:T(8,128)(2,1)S(1)} %bitcast_dynamic-update-slice_fusion.8) | copy-start | bytes 14155780 | tf_op jit(solution)/shard_map/while
  286.0 3.7 slice-start.2
  293.4 10.1 %copy-start.13 = (bf16[3,1024,12,64]{1,3,2,0:T(8,128)(2,1)}, bf16[3,1024,12,64]{1,3,2,0:T(8,128)(2,1)S(1)}, u32[]{:S(2)}) copy-start(bf16[3,1024,12,64]{1,3,2,0:T(8,128)(2,1)S(1)} %bitcast_dynamic-update-slice_fusion.8) | copy-start | bytes 14155780 | tf_op jit(solution)/shard_map/while
  325.5 10.1 %copy-start.13 = (bf16[3,1024,12,64]{1,3,2,0:T(8,128)(2,1)}, bf16[3,1024,12,64]{1,3,2,0:T(8,128)(2,1)S(1)}, u32[]{:S(2)}) copy-start(bf16[3,1024,12,64]{1,3,2,0:T(8,128)(2,1)S(1)} %bitcast_dynamic-update-slice_fusion.8) | copy-start | bytes 14155780 | tf_op jit(solution)/shard_map/while
  349.5 99.1 %reduce-scatter.5.cloned.1.call-start = ((), (), s32[]{:S(2)}) async-start(), calls=%async_computation.4 | async-start | bytes 5898240 | tf_op jit(solution)/shard_map/reduce_scatter | solution.py:607
  352.9 5.5 copy-start.38
  363.7 4.3 copy-start.34
  363.7 4.3 copy-start.40
  363.7 4.3 copy-start.45
  368.0 30.4 %copy-start.26 = (f32[256,64]{0,1:T(8,128)S(1)}, f32[256,64]{0,1:T(8,128)}, u32[]{:S(2)}) copy-start(f32[256,64]{0,1:T(8,128)} %copy-done.25) | copy-start | bytes 196612
  454.9 5.0 copy-start.16
  459.9 85.2 %copy-start.3 = (bf16[3,256,768]{2,1,0:T(8,128)(2,1)S(1)}, bf16[3,256,768]{2,1,0:T(8,128)(2,1)}, u32[]{:S(2)}) copy-start(bf16[3,256,768]{2,1,0:T(8,128)(2,1)} %param.11) | copy-start | bytes 3538948
  459.9 85.2 %copy-start.15 = (bf16[32,24,2304]{2,1,0:T(8,128)(2,1)S(1)}, bf16[32,24,2304]{2,1,0:T(8,128)(2,1)}, u32[]{:S(2)}) copy-start(bf16[32,24,2304]{2,1,0:T(8,128)(2,1)} %get-tuple-element.132) | copy-start | bytes 10616836
  550.6 4.2 copy-start.29
  (32 other events, 74.1 us)
Sparse Core Ops, SparseCore 0:
  56.2 62.8 all-gather.5
  120.6 41.0 all-gather.3
  348.2 50.1 reduce-scatter.2
  400.8 47.7 reduce-scatter.4

commit v2 on v1

--- a/solution.py
+++ b/solution.py
@@ -460,25 +460,348 @@
     return (grad_in - mean_grad - normed * mean_prod) * inverse
 
 
+def swap_halves(values):
+    lane = lax.broadcasted_iota(jnp.int32, values.shape, 1)
+    half = HEAD_DIM // 2
+    return jnp.where(
+        lane % HEAD_DIM < half, pltpu.roll(values, 128 - half, 1), pltpu.roll(values, half, 1)
+    )
+
+
 def rope_tables(positions):
     exponent = jnp.arange(HEAD_DIM // 2, dtype=jnp.float32) * (2.0 / HEAD_DIM)
     frequency = 10000.0 ** (-exponent)
     angles = positions.astype(jnp.float32)[:, None] * frequency[None, :]
-    cosine = jnp.concatenate([jnp.cos(angles), jnp.cos(angles)], -1)
-    sine_table = jnp.concatenate([jnp.sin(angles), jnp.sin(angles)], -1)
-    return (cosine[None, :, None, :], sine_table[None, :, None, :])
-
-
-def rotate(values, cosine, sine_table):
-    half_dim = values.shape[-1] // 2
-    turned = jnp.concatenate([-values[..., half_dim:], values[..., :half_dim]], -1)
-    return values * cosine + turned * sine_table
-
-
-def rotate_back(grad_in, cosine, sine_table):
-    half_dim = grad_in.shape[-1] // 2
-    scaled = grad_in * sine_table
-    return grad_in * cosine + jnp.concatenate([scaled[..., half_dim:], -scaled[..., :half_dim]], -1)
+    cosine, sine = jnp.cos(angles), jnp.sin(angles)
+    return jnp.concatenate([cosine] * 4, -1), jnp.concatenate([-sine, sine, -sine, sine], -1)
+
+
+def project_kernel(slots, scale, n_ref, w_ref, cos_ref, sin_ref, q_ref, kv_ref):
+    j = pl.program_id(0)
+    cosine, sine = cos_ref[...], sin_ref[...]
+    local = cosine.shape[0]
+    for s in range(slots):
+        rows = pl.ds(s * local, local)
+        part = jnp.dot(n_ref[rows, :], w_ref[...], preferred_element_type=jnp.float32)
+        for g in range(part.shape[1] // 128):
+            cols = pl.ds(g * 128, 128)
+            piece = part[:, g * 128:(g + 1) * 128]
+
+            @pl.when(j < 2)
+            def _():
+                turned = (piece * cosine + swap_halves(piece) * sine).astype(jnp.bfloat16)
+                q_ref[rows, cols] = (turned.astype(jnp.float32) * scale).astype(jnp.bfloat16)
+
+            @pl.when((j >= 2) & (j < 4))
+            def _():
+                kv_ref[rows, cols] = (piece * cosine + swap_halves(piece) * sine).astype(jnp.bfloat16)
+
+            @pl.when(j >= 4)
+            def _():
+                kv_ref[rows, cols] = piece.astype(jnp.bfloat16)
+
+
+def project_rows(normed, weight, cosine, sine, slots):
+    rows, width = normed.shape
+    tile = width // 2
+    return pl.pallas_call(
+        functools.partial(project_kernel, slots, HEAD_DIM ** -0.5),
+        grid=(6,),
+        out_shape=[jax.ShapeDtypeStruct((rows, width), jnp.bfloat16),
+                   jax.ShapeDtypeStruct((rows, 2 * width), jnp.bfloat16)],
+        in_specs=[pl.BlockSpec((rows, width), lambda j: (0, 0)),
+                  pl.BlockSpec((width, tile), lambda j: (0, j)),
+                  pl.BlockSpec(cosine.shape, lambda j: (0, 0)),
+                  pl.BlockSpec(sine.shape, lambda j: (0, 0))],
+        out_specs=[pl.BlockSpec((rows, tile), lambda j: (0, jnp.minimum(j, 1))),
+                   pl.BlockSpec((rows, tile), lambda j: (0, jnp.maximum(j - 2, 0)))],
+        compiler_params=pltpu.CompilerParams(vmem_limit_bytes=40 << 20),
+        name="project_rows",
+    )(normed, weight, cosine, sine)
+
+
+def chip_greet(o, i, y, c):
+    barrier = pltpu.get_barrier_semaphore()
+    for target in (device(o, i, 1 - y, c), device(o, i, y, 1 - c)):
+        pl.semaphore_signal(barrier, inc=1, device_id=target, device_id_type=MESH)
+    pl.semaphore_wait(barrier, 2)
+
+
+def share_kernel(slots, own_ref, all_ref, send, recv, local):
+    o, i, y, c = placement()
+    chip_greet(o, i, y, c)
+    mate, across = device(o, i, y, 1 - c), device(o, i, 1, c)
+    mine = y * 2 + c
+
+    def hop(kind, s, src, piece, target):
+        return pltpu.make_async_remote_copy(
+            src_ref=src, dst_ref=all_ref.at[piece, s], send_sem=send.at[kind, s],
+            recv_sem=recv.at[kind, s], device_id=target, device_id_type=MESH)
+
+    for s in range(slots):
+        @pl.when(y == 0)
+        def _(s=s):
+            hop(0, s, own_ref.at[s], mine, across).start()
+
+        hop(1, s, own_ref.at[s], mine, mate).start()
+        pltpu.make_async_copy(own_ref.at[s], all_ref.at[mine, s], local.at[s]).start()
+    for s in range(slots):
+        @pl.when(y == 1)
+        def _(s=s):
+            hop(0, s, own_ref.at[s], c, mate).wait_recv()
+            hop(2, s, all_ref.at[c, s], c, mate).start()
+    for s in range(slots):
+        hop(1, s, own_ref.at[s], y * 2 + 1 - c, mate).wait_recv()
+        hop(1, s, own_ref.at[s], mine, mate).wait_send()
+        pltpu.make_async_copy(own_ref.at[s], all_ref.at[mine, s], local.at[s]).wait()
+
+        @pl.when(y == 0)
+        def _(s=s):
+            hop(0, s, own_ref.at[s], mine, across).wait_send()
+
+        @pl.when(y == 1)
+        def _(s=s):
+            hop(2, s, all_ref.at[1 - c, s], 1 - c, mate).wait_recv()
+            hop(2, s, all_ref.at[c, s], c, mate).wait_send()
+
+
+def share_keys(own, collective_id):
+    slots = own.shape[0]
+    return pl.pallas_call(
+        functools.partial(share_kernel, slots),
+        out_shape=jax.ShapeDtypeStruct((4,) + own.shape, own.dtype),
+        in_specs=[pl.BlockSpec(memory_space=pl.ANY)],
+        out_specs=pl.BlockSpec(memory_space=pl.ANY),
+        scratch_shapes=[pltpu.SemaphoreType.DMA((3, slots)), pltpu.SemaphoreType.DMA((3, slots)),
+                        pltpu.SemaphoreType.DMA((slots,))],
+        compiler_params=pltpu.CompilerParams(collective_id=collective_id, has_side_effects=True),
+        name="share_keys",
+    )(own)
+
+
+def collect_kernel(slots, width, dk_ref, dv_ref, cos_ref, sin_ref, out_ref,
+                   own, mate_buf, far_mine, far_mate, far_sum, far_buf, send, recv, local):
+    o, i, y, c = placement()
+    chip_greet(o, i, y, c)
+    mate, across = device(o, i, y, 1 - c), device(o, i, 0, c)
+    mine, other = y * 2 + c, y * 2 + 1 - c
+    parts = (dk_ref, dv_ref)
+
+    def hop(kind, s, p, src, dst, target):
+        return pltpu.make_async_remote_copy(
+            src_ref=src, dst_ref=dst, send_sem=send.at[kind, s, p], recv_sem=recv.at[kind, s, p],
+            device_id=target, device_id_type=MESH)
+
+    def near(s, p):
+        return hop(0, s, p, parts[p].at[other, s], mate_buf.at[s, p], mate)
+
+    def far(s, p):
+        return hop(1, s, p, parts[p].at[1 - c, s], far_mate.at[s, p], mate)
+
+    def back(s, p):
+        return hop(2, s, p, far_sum.at[s, p], far_buf.at[s, p], across)
+
+    def load(s, p):
+        return pltpu.make_async_copy(parts[p].at[mine, s], own.at[s, p], local.at[0, s, p])
+
+    def load_far(s, p):
+        return pltpu.make_async_copy(parts[p].at[c, s], far_mine.at[s, p], local.at[1, s, p])
+
+    every = [(s, p) for s in range(slots) for p in range(2)]
+    for s, p in every:
+        @pl.when(y == 1)
+        def _(s=s, p=p):
+            far(s, p).start()
+            load_far(s, p).start()
+
+        near(s, p).start()
+        load(s, p).start()
+    for s, p in every:
+        @pl.when(y == 1)
+        def _(s=s, p=p):
+            far(s, p).wait_recv()
+            load_far(s, p).wait()
+            far_sum[s, p] = (far_mine[s, p].astype(jnp.float32)
+                             + far_mate[s, p].astype(jnp.float32)).astype(jnp.bfloat16)
+            back(s, p).start()
+
+    cosine, sine = cos_ref[...], sin_ref[...]
+
+    def put(s, p, total):
+        for g in range(width // 128):
+            cols = slice(g * 128, (g + 1) * 128)
+            piece = total[:, cols]
+            if p == 0:
+                piece = piece * cosine - swap_halves(piece) * sine
+            out_ref[s, :, pl.ds(p * width + g * 128, 128)] = piece.astype(jnp.bfloat16)
+
+    for s, p in every:
+        near(s, p).wait_recv()
+        load(s, p).wait()
+
+        @pl.when(y == 0)
+        def _(s=s, p=p):
+            back(s, p).wait_recv()
+            put(s, p, own[s, p].astype(jnp.float32) + mate_buf[s, p].astype(jnp.float32)
+                + far_buf[s, p].astype(jnp.float32))
+
+        @pl.when(y == 1)
+        def _(s=s, p=p):
+            put(s, p, own[s, p].astype(jnp.float32) + mate_buf[s, p].astype(jnp.float32))
+
+    for s, p in every:
+        near(s, p).wait_send()
+
+        @pl.when(y == 1)
+        def _(s=s, p=p):
+            far(s, p).wait_send()
+            back(s, p).wait_send()
+
+
+def collect_keys(dk, dv, cosine, sine, collective_id):
+    _, slots, local, width = dk.shape
+    buffer = pltpu.VMEM((slots, 2, local, width), jnp.bfloat16)
+    return pl.pallas_call(
+        functools.partial(collect_kernel, slots, width),
+        out_shape=jax.ShapeDtypeStruct((slots, local, 2 * width), jnp.bfloat16),
+        in_specs=[pl.BlockSpec(memory_space=pl.ANY)] * 2 + [pl.BlockSpec(memory_space=pltpu.VMEM)] * 2,
+        out_specs=pl.BlockSpec(memory_space=pltpu.VMEM),
+        scratch_shapes=[buffer] * 6 + [pltpu.SemaphoreType.DMA((3, slots, 2))] * 2
+        + [pltpu.SemaphoreType.DMA((2, slots, 2))],
+        compiler_params=pltpu.CompilerParams(collective_id=collective_id, has_side_effects=True, vmem_limit_bytes=40 << 20),
+        name="collect_keys",
+    )(dk, dv, cosine, sine)
+
+
+def masked_scores(query, keys, offset, length):
+    scores = lax.dot_general(query, keys, (((1,), (1,)), ((), ())), preferred_element_type=jnp.float32)
+    rows = lax.broadcasted_iota(jnp.int32, scores.shape, 0) + offset
+    cols = lax.broadcasted_iota(jnp.int32, scores.shape, 1)
+    return jnp.where((cols <= rows) & (cols < length), scores, -1e30)
+
+
+def one_head(values, h):
+    lane = lax.broadcasted_iota(jnp.int32, values.shape, 1)
+    keep = (lane < HEAD_DIM) if h == 0 else (lane >= HEAD_DIM)
+    return jnp.where(keep, values, jnp.zeros_like(values))
+
+
+def join_heads(first, second):
+    lane = lax.broadcasted_iota(jnp.int32, first.shape, 1)
+    return jnp.where(lane < HEAD_DIM, first, second)
+
+
+def forward_kernel(pieces, lens_ref, seq_ref, q_ref, k_ref, v_ref, o_ref, log_ref):
+    s = pl.program_id(0)
+    local = q_ref.shape[1]
+    length, seq = lens_ref[s], seq_ref[0]
+    live = seq * local < length
+
+    @pl.when(jnp.logical_not(live))
+    def _():
+        o_ref[...] = jnp.zeros_like(o_ref)
+        log_ref[...] = jnp.zeros_like(log_ref)
+
+    for n in range(1, pieces + 1):
+        @pl.when(live & (seq == n - 1))
+        def _(n=n):
+            query = q_ref[0]
+            keys = k_ref[:n, 0].reshape(n * local, 128)
+            values = v_ref[:n, 0].reshape(n * local, 128)
+            mixed, logs = [], []
+            for h in range(2):
+                scores = masked_scores(one_head(query, h), keys, (n - 1) * local, length)
+                top = jnp.max(scores, axis=1, keepdims=True)
+                terms = jnp.exp(scores - top)
+                total = jnp.sum(terms, axis=1, keepdims=True)
+                mix = jnp.dot(terms.astype(jnp.bfloat16), values, preferred_element_type=jnp.float32)
+                mixed.append(mix / total)
+                logs.append(jnp.broadcast_to(top + jnp.log(total), (local, 128)))
+            o_ref[0] = join_heads(*mixed).astype(jnp.bfloat16)
+            log_ref[0] = join_heads(*logs)
+
+
+def backward_kernel(pieces, scale, lens_ref, seq_ref, q_ref, k_ref, v_ref, do_ref, log_ref, cos_ref, sin_ref,
+                    dq_ref, dk_ref, dv_ref):
+    s = pl.program_id(0)
+    local = q_ref.shape[1]
+    length, seq = lens_ref[s], seq_ref[0]
+    live = seq * local < length
+
+    @pl.when(jnp.logical_not(live))
+    def _():
+        dq_ref[...] = jnp.zeros_like(dq_ref)
+        dk_ref[...] = jnp.zeros_like(dk_ref)
+        dv_ref[...] = jnp.zeros_like(dv_ref)
+
+    def across(left, right):
+        return lax.dot_general(left, right, (((0,), (0,)), ((), ())), preferred_element_type=jnp.float32)
+
+    for n in range(1, pieces + 1):
+        @pl.when(live & (seq == n - 1))
+        def _(n=n):
+            query, grad = q_ref[0], do_ref[0]
+            keys = k_ref[:n, 0].reshape(n * local, 128)
+            values = v_ref[:n, 0].reshape(n * local, 128)
+            dq, dk, dv = [], [], []
+            for h in range(2):
+                scores = masked_scores(one_head(query, h), keys, (n - 1) * local, length)
+                probs = jnp.exp(scores - log_ref[0, :, h * HEAD_DIM:h * HEAD_DIM + 1])
+                dprobs = lax.dot_general(one_head(grad, h), values, (((1,), (1,)), ((), ())),
+                                         preferred_element_type=jnp.float32)
+                inner = jnp.sum(probs * dprobs, axis=1, keepdims=True)
+                dscores = (probs * (dprobs - inner)).astype(jnp.bfloat16)
+                dq.append(jnp.dot(dscores, keys, preferred_element_type=jnp.float32))
+                dk.append(across(dscores, query))
+                dv.append(across(probs.astype(jnp.bfloat16), grad))
+            turn = join_heads(*dq) * scale
+            dq_ref[0] = (turn * cos_ref[...] - swap_halves(turn) * sin_ref[...]).astype(jnp.bfloat16)
+            dk_ref[:n, 0] = join_heads(*dk).astype(jnp.bfloat16).reshape(n, local, 128)
+            dv_ref[:n, 0] = join_heads(*dv).astype(jnp.bfloat16).reshape(n, local, 128)
+            if n < pieces:
+                rest = jnp.zeros((pieces - n, local, 128), jnp.bfloat16)
+                dk_ref[n:, 0] = rest
+                dv_ref[n:, 0] = rest
+
+
+def attend_specs(pieces, local, pairs):
+    row = pl.BlockSpec((1, local, 128), lambda s, h, *_: (s, 0, h))
+    key = pl.BlockSpec((pieces, 1, local, 128), lambda s, h, *_: (0, s, 0, h))
+    value = pl.BlockSpec((pieces, 1, local, 128), lambda s, h, *_: (0, s, 0, h + pairs))
+    return row, key, value
+
+
+def attend(query, kv_all, lengths):
+    slots, local, width = query.shape
+    pieces, pairs = kv_all.shape[0], width // 128
+    row, key, value = attend_specs(pieces, local, pairs)
+    seq = lax.axis_index("seq").astype(jnp.int32)[None]
+    return pl.pallas_call(
+        functools.partial(forward_kernel, pieces),
+        grid_spec=pltpu.PrefetchScalarGridSpec(
+            num_scalar_prefetch=2, grid=(slots, pairs), in_specs=[row, key, value], out_specs=[row, row]),
+        out_shape=[jax.ShapeDtypeStruct(query.shape, jnp.bfloat16), jax.ShapeDtypeStruct(query.shape, jnp.float32)],
+        compiler_params=pltpu.CompilerParams(vmem_limit_bytes=40 << 20),
+        name="attend",
+    )(lengths, seq, query, kv_all, kv_all)
+
+
+def attend_back(query, kv_all, grad, log_total, lengths, cosine, sine):
+    slots, local, width = query.shape
+    pieces, pairs = kv_all.shape[0], width // 128
+    row, key, value = attend_specs(pieces, local, pairs)
+    table = pl.BlockSpec(cosine.shape, lambda s, h, *_: (0, 0))
+    seq = lax.axis_index("seq").astype(jnp.int32)[None]
+    shared = jax.ShapeDtypeStruct((pieces, slots, local, width), jnp.bfloat16)
+    return pl.pallas_call(
+        functools.partial(backward_kernel, pieces, HEAD_DIM ** -0.5),
+        grid_spec=pltpu.PrefetchScalarGridSpec(
+            num_scalar_prefetch=2, grid=(slots, pairs),
+            in_specs=[row, key, value, row, row, table, table], out_specs=[row, key, key]),
+        out_shape=[jax.ShapeDtypeStruct(query.shape, jnp.bfloat16), shared, shared],
+        compiler_params=pltpu.CompilerParams(vmem_limit_bytes=48 << 20),
+        name="attend_back",
+    )(lengths, seq, query, kv_all, kv_all, grad, log_total, cosine, sine)
 
 
 def contract_last(left_side, right_side):
@@ -501,75 +824,18 @@
 
 def on_device(tokens, lengths, w_qkv, w_att_out, w_ffin, w_ffout, cotangent):
     slot_count, local_len, model_width = tokens.shape
-    head_count = model_width // HEAD_DIM
     row_count = slot_count * local_len
-    slot_len = local_len * lax.axis_size("seq")
     positions = lax.axis_index("seq") * local_len + jnp.arange(local_len, dtype=jnp.int32)
-    key_positions = jnp.arange(slot_len, dtype=jnp.int32)
     valid_rows = (positions[None, :] < lengths[:, None]).astype(jnp.float32)[:, :, None]
     cosine, sine_table = rope_tables(positions)
-    score_scale = HEAD_DIM ** (-0.5)
-
-    def masked_scores(query_one, key_one, length):
-        allowed = (key_positions[None, :] <= positions[:, None]) & (key_positions[None, :] < length)
-        raw_scores = (
-            jnp.einsum("qhd,khd->hqk", query_one, key_one, preferred_element_type=jnp.float32)
-            * score_scale
-        )
-        return jnp.where(allowed[None], raw_scores, -1e30)
-
-    def forward_slot(item):
-        query_one, key_one, value_one, length = item
-        scores = masked_scores(query_one, key_one, length)
-        row_top = jnp.max(scores, axis=-1, keepdims=True)
-        exponent_terms = jnp.exp(scores - row_top)
-        row_total = jnp.sum(exponent_terms, axis=-1, keepdims=True)
-        probs_bf = (exponent_terms / row_total).astype(jnp.bfloat16)
-        mixed_one = jnp.einsum(
-            "hqk,khd->qhd", probs_bf, value_one, preferred_element_type=jnp.float32
-        )
-        return (mixed_one.astype(jnp.bfloat16), row_top + jnp.log(row_total))
-
-    def backward_slot(item):
-        query_one, key_one, value_one, grad_mixed_one, log_one, length = item
-        probs_again = jnp.exp(masked_scores(query_one, key_one, length) - log_one)
-        probs_again_bf = probs_again.astype(jnp.bfloat16)
-        grad_probs = jnp.einsum(
-            "qhd,khd->hqk", grad_mixed_one, value_one, preferred_element_type=jnp.float32
-        )
-        grad_scores = probs_again * (
-            grad_probs - jnp.sum(probs_again * grad_probs, axis=-1, keepdims=True)
-        )
-        grad_scores_bf = grad_scores.astype(jnp.bfloat16)
-        grad_query_one = (
-            jnp.einsum("hqk,khd->qhd", grad_scores_bf, key_one, preferred_element_type=jnp.float32)
-            * score_scale
-        )
-        grad_key_one = (
-            jnp.einsum(
-                "hqk,qhd->khd", grad_scores_bf, query_one, preferred_element_type=jnp.float32
-            )
-            * score_scale
-        )
-        grad_value_one = jnp.einsum(
-            "hqk,qhd->khd", probs_again_bf, grad_mixed_one, preferred_element_type=jnp.float32
-        )
-        return (grad_query_one, grad_key_one, grad_value_one)
-
     inputs = tokens.astype(jnp.float32).reshape(row_count, model_width)
     normed_one, inverse_one = norm_rows(inputs)
     normed_one_bf = normed_one.astype(jnp.bfloat16)
     qkv_full, att_out_full = gather_weights(w_qkv, w_att_out, 1)
-    project = jnp.dot(normed_one_bf, qkv_full, preferred_element_type=jnp.float32)
-    project = project.reshape(slot_count, local_len, 3, head_count, HEAD_DIM)
-    query_bf = rotate(project[:, :, 0], cosine, sine_table).astype(jnp.bfloat16)
-    key_bf = rotate(project[:, :, 1], cosine, sine_table).astype(jnp.bfloat16)
-    value_bf = project[:, :, 2].astype(jnp.bfloat16)
-    key_all, value_all = (
-        lax.all_gather(key_bf, "seq", axis=1, tiled=True),
-        lax.all_gather(value_bf, "seq", axis=1, tiled=True),
-    )
-    mixed_slots, log_total = lax.map(forward_slot, (query_bf, key_all, value_all, lengths))
+    query_rows, kv_rows = project_rows(normed_one_bf, qkv_full, cosine, sine_table, slot_count)
+    query_bf = query_rows.reshape(tokens.shape)
+    kv_all = share_keys(kv_rows.reshape(slot_count, local_len, 2 * model_width), 4)
+    mixed_slots, log_total = attend(query_bf, kv_all, lengths)
     mixed_bf = mixed_slots.reshape(row_count, model_width)
     hidden_state = inputs + jnp.dot(mixed_bf, att_out_full, preferred_element_type=jnp.float32)
     normed_two, inverse_two = norm_rows(hidden_state)
@@ -595,28 +861,11 @@
     grad_hidden_bf = grad_hidden.astype(jnp.bfloat16)
     qkv_back, att_out_back = qkv_full, att_out_full
     grad_mixed_bf = contract_last(grad_hidden_bf, att_out_back).astype(jnp.bfloat16)
-    grad_mixed_bf = grad_mixed_bf.reshape(slot_count, local_len, head_count, HEAD_DIM)
-    key_use, value_use = (key_all, value_all)
-    grad_query, grad_key_all, grad_value_all = lax.map(
-        backward_slot, (query_bf, key_use, value_use, grad_mixed_bf, log_total, lengths)
+    grad_query, grad_key_all, grad_value_all = attend_back(
+        query_bf, kv_all, grad_mixed_bf.reshape(tokens.shape), log_total, lengths, cosine, sine_table
     )
-    grad_key, grad_value = (
-        lax.psum_scatter(
-            grad_key_all.astype(jnp.bfloat16), "seq", scatter_dimension=1, tiled=True
-        ).astype(jnp.float32),
-        lax.psum_scatter(
-            grad_value_all.astype(jnp.bfloat16), "seq", scatter_dimension=1, tiled=True
-        ).astype(jnp.float32),
-    )
-    grad_project_bf = jnp.stack(
-        [
-            rotate_back(grad_query, cosine, sine_table),
-            rotate_back(grad_key, cosine, sine_table),
-            grad_value,
-        ],
-        2,
-    )
-    grad_project_bf = grad_project_bf.reshape(row_count, 3 * model_width).astype(jnp.bfloat16)
+    grad_kv = collect_keys(grad_key_all, grad_value_all, cosine, sine_table, 5)
+    grad_project_bf = jnp.concatenate([grad_query, grad_kv], 2).reshape(row_count, 3 * model_width)
     grad_normed_one = contract_last(grad_project_bf, qkv_back)
     grad_tokens = grad_hidden + norm_back(grad_normed_one, normed_one, inverse_one)
     grad_qkv, grad_att_out, grad_ffin, grad_ffout = scatter_rows(

time: 571 us -> 470 us (0.82)
  Pallas kernels: 191 us -> 371 us
  matrix products: 161 us -> 56.9 us
  waiting for transfers between devices: 85.4 us -> 0 us
  other arithmetic: 58.6 us -> 9.98 us
  local copies, waits for them, and re-layouts: 51 us -> 23.5 us
  between operations: 14.8 us -> 1.55 us
    pallas_call x0 -> x5, Pallas kernels: none -> 188 us  [the longest x1 73.1 us: share_keys(): pl.pallas_call(functools.partial(share_kernel, slots), out_shape=jax.Shap...]
    dot_general x22 -> x0, matrix products: 102 us -> none  [the longest x3 30.2 us: backward_slot(): jnp.einsum('qhd,khd->hqk', grad_mixed_one, value_one, preferred_element_t...]
    reduce_scatter x2 -> x0, waiting for transfers between devices: 65.9 us -> none  [the longest x1 43.4 us: on_device(): lax.psum_scatter(grad_value_all.astype(jnp.bfloat16), 'seq', scatter_dime...]
    convert_element_type x4 -> x0, other arithmetic: 22.4 us -> none  [the longest x3 20.1 us: backward_slot(): grad_scores_bf = grad_scores.astype(jnp.bfloat16)]
    all_gather x2 -> x0, waiting for transfers between devices: 18.9 us -> none  [the longest x1 18.9 us: on_device(): lax.all_gather(key_bf, 'seq', axis=1, tiled=True)]
    pallas_call x2, Pallas kernels: 106 us -> 88.3 us  [gather_rows(): pl.pallas_call(kernel, out_shape=[jax.ShapeDtypeStruct((devices,) + v.sha...]
    reduce_sum x3 -> x0, other arithmetic: 10.9 us -> none  [forward_slot(): row_total = jnp.sum(exponent_terms, axis=-1, keepdims=True)]
    pallas_call x1, Pallas kernels: 85.2 us -> 94.4 us  [scatter_rows(): pl.pallas_call(kernel, out_shape=[jax.ShapeDtypeStruct(s, jnp.float32) fo...]
  transfers between devices with their start and end apart: 4 -> 0, of which waited for: 3 -> 0; matrix products, arithmetic and copies ran while one was open for 6% -> 0% of each run, Pallas kernels for 14% -> 0%
where the time goes in v2:
time: 470 us; the launch traced here: 463 us
  Pallas kernels  371 us (79%)
  matrix products  56.9 us (12%)
  local copies, waits for them, and re-layouts  23.5 us (5%)
  other arithmetic  9.98 us (2%)
    pallas_call x1, Pallas kernels, scatter_rows(): pl.pallas_call(kernel, out_shape=[jax.ShapeDtypeStruct(s, jnp.float32) fo...  94.4 us
    pallas_call x2, Pallas kernels, gather_rows(): pl.pallas_call(kernel, out_shape=[jax.ShapeDtypeStruct((devices,) + v.sha...  88.3 us
    pallas_call x1, Pallas kernels, share_keys(): pl.pallas_call(functools.partial(share_kernel, slots), out_shape=jax.Shap...  73.1 us
    pallas_call x1, Pallas kernels, collect_keys(): pl.pallas_call(functools.partial(collect_kernel, slots, width), out_shape...  62 us
    unnamed x84, local copies, waits for them, and re-layouts  23.5 us
    pallas_call x1, Pallas kernels, attend_back(): pl.pallas_call(functools.partial(backward_kernel, pieces, HEAD_DIM ** (-0...  23.4 us
    dot_general x4, matrix products, contract_last(): lax.dot_general(left_side, right_side, (((1,), (1,)), ((), ())), preferre...  23.3 us
    dot_general x4, matrix products, weight_term(): lax.dot_general(left_side, right_side, (((0,), (0,)), ((), ())), preferre...  19.1 us

profile of v2, /device:TPU:10, one launch (start us, length us, event | category | flops | bytes accessed | tf_op | source)
XLA Modules:
  0.0 462.5 jit_solution(4308836674120074261)
XLA Ops:
  2.0 1.5 convert_reduce_fusion
  5.2 29.7 %gather_rows.2 = (bf16[32,24,2304]{2,1,0:T(8,128)(2,1)}, bf16[32,24,768]{2,1,0:T(8,128)(2,1)}) custom-call(bf16[24,2304]{1,0:T(8,128)(2,1)} %refs_0_.2, bf16[24,768]{1,0:T(8,128)(2,1)} %refs_1_.2), custom_call_target="tpu_custom_call" | custom-call | tf_op jit(solution)/shard_map/gather_rows/pallas_call | solution.py:237
  34.9 2.0 copy-done.3
  36.9 13.1 %project_rows.1 = (bf16[768,768]{1,0:T(8,128)(2,1)S(1)}, bf16[768,1536]{1,0:T(8,128)(2,1)S(1)}) custom-call(bf16[768,768]{1,0:T(8,128)(2,1)S(1)} %fusion.8.n_ref, bf16[768,2304]{1,0:T(8,128)(2,1)S(1)} %bitcast.57, f32[256,128]{1,0:T(8,128)S(1)} %pad_maximum_fusion.4.cos_ref, f32[256,128]{1,0:T(8,128)S(1)} %pad_maximum_fusion.5.sin_ref), custom_call_target="tpu_custom_call" | custom-call | tf_op jit(solution)/shard_map/project_rows/pallas_call | solution.py:507
  50.0 1.4 copy-done.5
  51.4 73.1 %share_keys.1.k_ref.v_ref = bf16[4,3,256,1536]{3,2,1,0:T(8,128)(2,1)} custom-call(bf16[3,256,1536]{2,1,0:T(8,128)(2,1)} %bitcast.59), custom_call_target="tpu_custom_call" | custom-call | tf_op jit(solution)/shard_map/share_keys/pallas_call | solution.py:570
  124.6 3.7 copy-done
  128.2 16.3 %attend.1 = (bf16[3,256,768]{2,1,0:T(8,128)(2,1)S(1)}, f32[3,256,768]{2,1,0:T(8,128)S(1)}) custom-call(s32[3]{0:T(128)S(1)} %copy-done.10, s32[1]{0:T(128)} %bitcast.1.seq_ref, bf16[3,256,768]{2,1,0:T(8,128)(2,1)S(1)} %bitcast.55, bf16[4,3,256,1536]{3,2,1,0:T(8,128)(2,1)S(1)} %copy-done, bf16[4,3,256,1536]{3,2,1,0:T(8,128)(2,1)S(1)} %copy-done), custom_call_target="tpu_custom_call" | custom-call | tf_op jit(solution)/shard_map/attend/pallas_call | solution.py:779
  144.5 1.2 fusion.29
  145.8 1.4 copy-done.16
  148.2 58.6 %gather_rows.3 = (bf16[32,24,4096]{2,1,0:T(8,128)(2,1)}, bf16[32,64,768]{2,1,0:T(8,128)(2,1)}) custom-call(bf16[24,4096]{1,0:T(8,128)(2,1)} %refs_0_.3, bf16[64,768]{1,0:T(8,128)(2,1)} %refs_1_.3), custom_call_target="tpu_custom_call" | custom-call | tf_op jit(solution)/shard_map/gather_rows/pallas_call | solution.py:237
  206.9 10.7 %fusion.25 = f32[768,4096]{1,0:T(8,128)} fusion(bf16[768,4096]{1,0:T(8,128)(2,1)} %bitcast.71, f32[768,768]{1,0:T(8,128)} %copy-done.16, f32[768]{0:T(1024)} %add_rsqrt_fusion, f32[768]{0:T(1024)S(1)} %broadcast_multiply_fusion.4), kind=kOutput, calls=%fused_computation.61 | convolution fusion | flops 4833607680 | bytes 21239808 | tf_op jit(solution)/shard_map/dot_general | solution.py:844
  218.2 1.3 copy-done.34
  219.5 9.8 %multiply_convert_fusion.1 = (bf16[768,2048]{1,0:T(8,128)(2,1)S(1)}, bf16[768,2048]{1,0:T(8,128)(2,1)}, bf16[768,2048]{1,0:T(8,128)(2,1)}) fusion(f32[768,4096]{1,0:T(8,128)} %fusion.25, bf16[768,768]{1,0:T(8,128)(2,1)S(1)} %bitcast.70, bf16[2048,768]{1,0:T(8,128)(2,1)S(1)} %bitcast.73), kind=kOutput, calls=%fused_computation.4 | convolution fusion | flops 2441084928 | bytes 26345472 | tf_op jit(solution)/shard_map/dot_general | solution.py:808
  229.4 7.8 %convolution_convert_fusion = bf16[768,4096]{1,0:T(8,128)(2,1)} fusion(bf16[768,2048]{1,0:T(8,128)(2,1)} %get-tuple-element.41, bf16[768,2048]{1,0:T(8,128)(2,1)S(1)} %get-tuple-element.40, f32[768,768]{1,0:T(8,128)S(1)} %copy-done.17, f32[768]{0:T(1024)S(1)} %copy-done.30, f32[768]{0:T(1024)S(1)} %broadcast_multiply_fusion.4), kind=kOutput, calls=%fused_computation.1 | convolution fusion | flops 4849336320 | bytes 14948352 | tf_op jit(solution)/shard_map/dot_general | solution.py:819
  237.1 9.2 %fusion.28 = (f32[768]{0:T(1024)S(1)}, f32[768]{0:T(1024)S(1)}, f32[768,768]{1,0:T(8,128)S(1)}) fusion(f32[768]{0:T(1024)S(1)} %copy-done.30, f32[768,768]{1,0:T(8,128)S(1)} %copy-done.17, f32[768]{0:T(1024)S(1)} %broadcast_multiply_fusion.4, bf16[768,4096]{1,0:T(8,128)(2,1)} %bitcast.72, bf16[768,2048]{1,0:T(8,128)(2,1)} %get-tuple-element.41, ...), kind=kOutput, calls=%fused_computation.63 | convolution fusion | flops 4847368192 | bytes 17313792 | tf_op jit(solution)/shard_map/dot_general | solution.py:808
  247.7 1.1 convolution_convert_fusion.3
  249.1 23.4 %attend_back.1 = (bf16[3,256,768]{2,1,0:T(8,128)(2,1)S(1)}, bf16[4,3,256,768]{3,2,1,0:T(8,128)(2,1)}, bf16[4,3,256,768]{3,2,1,0:T(8,128)(2,1)}) custom-call(s32[3]{0:T(128)S(1)} %copy-done.10, s32[1]{0:T(128)} %bitcast.1.seq_ref, bf16[3,256,768]{2,1,0:T(8,128)(2,1)S(1)} %bitcast.56, bf16[4,3,256,1536]{3,2,1,0:T(8,128)(2,1)} %share_keys.1.k_ref.v_ref, ...), custom_call_target="tpu_custom_call" | custom-call | tf_op jit(solution)/shard_map/attend_back/pallas_call | solution.py:796
  272.5 2.3 copy-done.1
  274.9 2.3 copy-done.2
  277.2 62.0 %collect_keys.1 = bf16[3,256,1536]{2,1,0:T(8,128)(2,1)S(1)} custom-call(bf16[4,3,256,768]{3,2,1,0:T(8,128)(2,1)S(1)} %copy-done.1, bf16[4,3,256,768]{3,2,1,0:T(8,128)(2,1)S(1)} %copy-done.2, f32[256,128]{1,0:T(8,128)S(1)} %copy-done.9, f32[256,128]{1,0:T(8,128)S(1)} %copy-done.7), custom_call_target="tpu_custom_call" | custom-call | tf_op jit(solution)/shard_map/collect_keys/pallas_call | solution.py:664
  339.2 5.0 %bitcast_convert_fusion = bf16[768,2304]{1,0:T(8,128)(2,1)} fusion(bf16[3,256,768]{2,1,0:T(8,128)(2,1)S(1)} %copy-done.15, f32[3,256]{1,0:T(4,128)S(1)} %copy-done.32, f32[3,256]{1,0:T(4,128)S(1)} %copy-done.27, bf16[3,256,1536]{2,1,0:T(8,128)(2,1)S(1)} %collect_keys.1, bf16[3,256,768]{2,1,0:T(8,128)(2,1)S(1)} %get-tuple-element.29), kind=kOutput, calls=%fused_computation | convolution fusion | flops 2729115648 | bytes 8263680 | tf_op jit(solution)/shard_map/dot_general | solution.py:819
  344.3 2.1 convolution_convert_fusion.2
  346.5 1.8 copy-done.38
  348.3 4.2 convolution_convert_fusion.1
  352.5 94.4 %scatter_rows.1 = (f32[24,2304]{1,0:T(8,128)}, f32[24,768]{1,0:T(8,128)}, f32[24,4096]{1,0:T(8,128)}, f32[64,768]{1,0:T(8,128)}) custom-call(bf16[32,24,2304]{2,1,0:T(8,128)(2,1)} %bitcast.64, bf16[32,24,768]{2,1,0:T(8,128)(2,1)} %bitcast.69, bf16[32,24,4096]{2,1,0:T(8,128)(2,1)} %bitcast.63, bf16[32,64,768]{2,1,0:T(8,128)(2,1)} %bitcast.66), custom_call_target="tpu_custom_call" | custom-call | tf_op jit(solution)/shard_map/scatter_rows/pallas_call | solution.py:439
  447.1 1.8 copy-done.4
  448.8 3.1 fusion.27
  452.0 2.1 fusion.12
  454.2 1.3 copy-done.35
  455.5 2.6 convolution_add_fusion
  458.1 1.2 multiply_convert_fusion.3
  (97 shorter events, 9.3 us)
Async XLA Ops:
  0.6 2.9 copy-start.13
  2.0 32.9 %copy-start.6 = (f32[256,128]{1,0:T(8,128)}, f32[256,128]{1,0:T(8,128)S(1)}, u32[]{:S(2)}) copy-start(f32[256,128]{1,0:T(8,128)S(1)} %pad_maximum_fusion.5.sin_ref) | copy-start | bytes 393220
  3.5 46.4 %copy-start.26 = (f32[3,256]{1,0:T(4,128)}, f32[3,256]{1,0:T(4,128)S(1)}, u32[]{:S(2)}) copy-start(f32[3,256]{1,0:T(4,128)S(1)} %broadcast_multiply_fusion.5) | copy-start | bytes 9220
  5.2 44.8 %copy-start.8 = (f32[256,128]{1,0:T(8,128)}, f32[256,128]{1,0:T(8,128)S(1)}, u32[]{:S(2)}) copy-start(f32[256,128]{1,0:T(8,128)S(1)} %pad_maximum_fusion.4.cos_ref) | copy-start | bytes 393220
  34.9 2.0 copy-start.3
  50.0 1.4 copy-start.5
  51.4 73.2 %copy-start.10 = (s32[3]{0:T(128)S(1)}, s32[3]{0:T(128)}, u32[]{:S(2)}) copy-start(s32[3]{0:T(128)} %lens_ref.3) | copy-start | bytes 40
  124.5 3.7 copy-start
  128.2 16.3 %copy-start.14 = (bf16[3,256,768]{2,1,0:T(8,128)(2,1)S(1)}, bf16[3,256,768]{2,1,0:T(8,128)(2,1)}, u32[]{:S(2)}) copy-start(bf16[3,256,768]{2,1,0:T(8,128)(2,1)} %param.7) | copy-start | bytes 3538948
  128.2 16.3 %copy-start.36 = (bf16[32,24,768]{2,1,0:T(8,128)(2,1)S(1)}, bf16[32,24,768]{2,1,0:T(8,128)(2,1)}, u32[]{:S(2)}) copy-start(bf16[32,24,768]{2,1,0:T(8,128)(2,1)} %get-tuple-element.25) | copy-start | bytes 3538948
  145.7 1.4 copy-start.16
  206.8 10.7 %copy-start.33 = (s32[256]{0:T(256)S(1)}, s32[256]{0:T(256)}, u32[]{:S(2)}) copy-start(s32[256]{0:T(256)} %get-tuple-element.52) | copy-start | bytes 3076
  206.8 10.8 %copy-start.21 = (bf16[3,256,768]{2,1,0:T(8,128)(2,1)S(1)}, bf16[3,256,768]{2,1,0:T(8,128)(2,1)}, u32[]{:S(2)}) copy-start(bf16[3,256,768]{2,1,0:T(8,128)(2,1)} %param.13) | copy-start | bytes 3538948
  217.6 1.9 copy-start.34
  219.5 9.8 %copy-start.17 = (f32[768,768]{1,0:T(8,128)S(1)}, f32[768,768]{1,0:T(8,128)}, u32[]{:S(2)}) copy-start(f32[768,768]{1,0:T(8,128)} %copy-done.16) | copy-start | bytes 7077892
  219.5 9.8 %copy-start.30 = (f32[768]{0:T(1024)S(1)}, f32[768]{0:T(1024)}, u32[]{:S(2)}) copy-start(f32[768]{0:T(1024)} %add_rsqrt_fusion) | copy-start | bytes 9220
  272.5 2.3 copy-start.1
  274.9 2.3 copy-start.2
  277.2 62.0 %copy-start.15 = (bf16[3,256,768]{2,1,0:T(8,128)(2,1)S(1)}, bf16[3,256,768]{2,1,0:T(8,128)(2,1)}, u32[]{:S(2)}) copy-start(bf16[3,256,768]{2,1,0:T(8,128)(2,1)} %param.7) | copy-start | bytes 3538948
  277.2 62.0 %copy-start.27 = (f32[3,256]{1,0:T(4,128)S(1)}, f32[3,256]{1,0:T(4,128)}, u32[]{:S(2)}) copy-start(f32[3,256]{1,0:T(4,128)} %copy-done.26) | copy-start | bytes 9220
  277.2 62.0 %copy-start.32 = (f32[3,256]{1,0:T(4,128)S(1)}, f32[3,256]{1,0:T(4,128)}, u32[]{:S(2)}) copy-start(f32[3,256]{1,0:T(4,128)} %copy-done.31) | copy-start | bytes 9220
  339.2 5.1 %copy-start.12 = (bf16[3,256,768]{2,1,0:T(8,128)(2,1)S(1)}, bf16[3,256,768]{2,1,0:T(8,128)(2,1)}, u32[]{:S(2)}) copy-start(bf16[3,256,768]{2,1,0:T(8,128)(2,1)} %copy-done.11) | copy-start | bytes 3538948
  339.2 5.0 %copy-start.20 = (f32[768,768]{1,0:T(8,128)S(1)}, f32[768,768]{1,0:T(8,128)}, u32[]{:S(2)}) copy-start(f32[768,768]{1,0:T(8,128)} %copy-done.19) | copy-start | bytes 7077892
  346.4 1.9 copy-start.38
  446.8 2.0 copy-start.4
  448.8 5.3 %copy-start.39 = (bf16[768,2048]{1,0:T(8,128)(2,1)S(1)}, bf16[768,2048]{1,0:T(8,128)(2,1)}, u32[]{:S(2)}) copy-start(bf16[768,2048]{1,0:T(8,128)(2,1)} %get-tuple-element.42) | copy-start | bytes 9437188
  452.0 2.2 copy-start.18
  452.0 3.4 copy-start.35
  455.5 2.7 copy-start.29
  458.1 1.9 copy-start.25
  458.1 2.6 copy-start.22
  458.1 3.3 copy-start.24
  (8 other events, 9.2 us)
